TPU v7x, 512 devices: a 4x2x32 block of a 4x8x32 slice. The times are simulated.
512 devices in a mesh: groups: 2 (over y), dp: 4 (over x), tensor: 64 (over z, core).
Axes of the slice: x: 4, y: 2, z: 32, core: 2. Of those that a mesh axis runs over, the one named last changes fastest.
The devices are a block of a 4x8x32 slice.
Arguments:
- tokens: bfloat16 [1024, 8192], P(('groups', 'dp'), 'tensor'), parts along dimension 0, may hold values from -6 to 6
- gate_up_weight: bfloat16 [8192, 32768], P('dp', 'tensor'), may hold values from -0.0625 to 0.0625
- down_weight: bfloat16 [16384, 8192], P('tensor', 'dp'), may hold values from -0.046875 to 0.046875
Outputs:
- mixed_out: bfloat16 [1024, 8192], P(('groups', 'dp'), 'tensor'), parts along dimension 0
There are 2 independent parts, one for each index of `groups`. A program takes and returns all parts, laid end to end along the dimension named above; an argument that names none is the same for every part. Nothing has to cross between parts.
All inputs are finite; a program needn't handle non-finite values.
Results may differ from a plain program's by a relative error of at most 0.0049.
Values may be sent and summed in bfloat16 or wider, within the bound.
No kernel may reach another device: no remote copies, remote signals or barrier semaphores. Data moves between devices by JAX's collectives and lax.ppermute only.
A program may use at most 64 MiB of HBM per device.

v0:
```python
import jax
import jax.numpy as jnp
from jax import lax
from jax.sharding import Mesh
from jax.sharding import PartitionSpec as P

TENSOR = ("tensor_0", "tensor_1")


def split_up(array, dim, devices):
    lengths = array.shape
    pieces = array.reshape(*lengths[:dim], devices, lengths[dim] // devices, *lengths[dim + 1 :])
    return jnp.moveaxis(pieces, dim, 0)


def summed_on_arrival(array, axis, dim):
    pieces = split_up(array, dim, lax.axis_size(axis))
    arrived = lax.all_to_all(pieces, axis, split_axis=0, concat_axis=0, tiled=True)
    return arrived.sum(axis=0)


def reduced_to_own(pieces, axes, turns):
    lengths = [lax.axis_size(a) for a in axes]
    pieces = pieces.reshape(*lengths, *pieces.shape[1:])
    pieces = pieces.transpose(*turns, *range(len(axes), pieces.ndim))
    pieces = pieces.reshape(-1, *pieces.shape[len(axes) :])
    for k in turns:
        pieces = lax.psum_scatter(pieces, axes[k], scatter_dimension=0, tiled=True)
    return pieces[0]


def summed_rows(array, axes, turns, dim):
    devices = lax.axis_size(axes)
    return reduced_to_own(split_up(array, dim, devices), axes, turns)


def per_device(tokens, gate_up_weight, down_weight):
    whole = lax.all_gather(tokens, TENSOR, axis=1, tiled=True)
    blocks = lax.all_to_all(whole, "dp", split_axis=1, concat_axis=0, tiled=True)
    partial_value = jnp.dot(blocks, gate_up_weight, preferred_element_type=jnp.float32)
    combined = summed_on_arrival(partial_value, "dp", 0)
    gate_part = combined[:, 0::2]
    up_part = combined[:, 1::2]
    hidden = (jax.nn.silu(gate_part) * up_part).astype(jnp.bfloat16)
    terms = jnp.dot(
        hidden,
        lax.all_gather(down_weight, "dp", axis=1, tiled=True),
        preferred_element_type=jnp.float32,
    )
    result = summed_rows(terms, TENSOR, (1, 0), 1).astype(jnp.bfloat16)
    return result


def solution(mesh):
    split = Mesh(
        mesh.devices.reshape(mesh.shape["groups"], mesh.shape["dp"], 32, 2),
        ("groups", "dp", "tensor_0", "tensor_1"),
    )
    placed = (P(("groups", "dp"), TENSOR), P("dp", TENSOR), P(TENSOR, "dp"))
    return jax.shard_map(
        per_device,
        mesh=split,
        in_specs=placed,
        out_specs=P(("groups", "dp"), TENSOR),
        check_vma=False,
    )
```

profile of v0, /device:TPU:34, one launch (start us, length us, event | category | flops | bytes accessed | tf_op | source)
XLA Modules:
  0.0 427.3 jit_solution(7535571929986580808)
XLA Ops:
  6.5 0.0 copy-start
  6.6 0.0 all-gather.3.cloned.1.call-start
  6.6 1.6 copy.5
  8.2 0.1 all-gather.3.cloned.1.call-update
  8.2 0.1 all-gather.5.cloned.1.call-start
  8.3 0.7 all-gather.5.cloned.1.call-update
  9.1 0.1 reduce-scatter.3.cloned.1.call-start
  9.1 160.0 %all-gather.3.cloned.1.call-done = bf16[128,8192]{0,1:T(8,128)(2,1)} async-done(((bf16[128,128]{0,1:T(8,128)(2,1)}), bf16[128,8192]{0,1:T(8,128)(2,1)}) %all-gather.3.cloned.1.call-update) | async-done | bytes 2097168 | tf_op jit(solution)/shard_map/all_gather | solution.py:38
  169.1 4.0 copy.6
  173.1 41.2 %all_to_all.21 = bf16[128,4,2048]{2,0,1:T(8,128)(2,1)S(1)} all-to-all(bf16[128,4,2048]{2,0,1:T(8,128)(2,1)} %copy.6), channel_id=1, replica_groups=mesh['groups'=2,'dp'=4,'tensor_0'=32,'tensor_1'=2] {'dp'}, dimensions={1} | all-to-all | bytes 4194304 | tf_op jit(solution)/shard_map/all_to_all | solution.py:39
  214.3 0.0 copy-done
  214.3 1.2 fusion
  215.5 29.6 %all_to_all.22 = f32[4,128,512]{2,1,0:T(8,128)S(1)} all-to-all(f32[4,128,512]{2,1,0:T(8,128)S(1)} %fusion), channel_id=1, replica_groups=mesh['groups'=2,'dp'=4,'tensor_0'=32,'tensor_1'=2] {'dp'}, dimensions={0} | all-to-all | bytes 2097152 | tf_op jit(solution)/shard_map/all_to_all | solution.py:18
  245.1 0.1 reduce_sum.9
  245.2 4.5 %slice.7 = f32[128,256]{1,0:T(8,128)S(1)} slice(f32[128,512]{1,0:T(8,128)S(1)} %reduce_sum.9), slice={[0:128:1], [1:512:2]} | slice | bytes 262144 | tf_op jit(solution)/shard_map/slice | solution.py:43
  249.7 4.5 %slice.6 = f32[128,256]{1,0:T(8,128)S(1)} slice(f32[128,512]{1,0:T(8,128)S(1)} %reduce_sum.9), slice={[0:128:1], [0:512:2]} | slice | bytes 262144 | tf_op jit(solution)/shard_map/slice | solution.py:42
  254.2 0.0 all-gather.5.cloned.1.call-done
  254.2 2.9 convolution_bitcast_fusion
  257.2 0.7 copy.8
  257.9 4.4 %copy.7 = f32[32,2,128,128]{3,2,0,1:T(8,128)} copy(f32[32,2,128,128]{3,1,0,2:T(2,128)S(1)} %bitcast.21) | data formatting | bytes 8388608 | tf_op jit(solution)/shard_map/reshape | solution.py:24
  262.3 0.1 reduce-scatter.3.cloned.1.call-update
  262.3 0.1 reduce-scatter.5.cloned.1.call-start
  262.4 15.9 %reduce-scatter.3.cloned.1.call-done = f32[32,128,128]{2,1,0:T(8,128)} async-done(((f32[64,128,128]{2,1,0:T(8,128)}), f32[32,128,128]{2,1,0:T(8,128)}) %reduce-scatter.3.cloned.1.call-update) | async-done | bytes 2097168 | tf_op jit(solution)/shard_map/reduce_scatter | solution.py:28
  278.3 0.1 reduce-scatter.5.cloned.1.call-update
  278.4 141.0 %reduce-scatter.5.cloned.1.call-done = f32[1,128,128]{2,1,0:T(8,128)} async-done(((f32[32,128,128]{2,1,0:T(8,128)}), f32[1,128,128]{2,1,0:T(8,128)}) %reduce-scatter.5.cloned.1.call-update) | async-done | bytes 65552 | tf_op jit(solution)/shard_map/reduce_scatter | solution.py:28
  419.3 1.5 convert_bitcast_fusion
Async XLA Ops:
  6.5 207.8 %copy-start = (bf16[2048,512]{1,0:T(8,128)(2,1)S(1)}, bf16[2048,512]{1,0:T(8,128)(2,1)}, u32[]{:S(2)}) copy-start(bf16[2048,512]{1,0:T(8,128)(2,1)} %param.4) | copy-start | bytes 6291460
  6.6 162.5 %all-gather.3.cloned.1.call-start = ((), (), s32[]{:S(2)}) async-start(), calls=%async_computation.4 | async-start | bytes 2129920 | tf_op jit(solution)/shard_map/all_gather | solution.py:38
  8.2 246.0 %all-gather.5.cloned.1.call-start = ((), (), s32[]{:S(2)}) async-start(), calls=%async_computation.5 | async-start | bytes 5242880 | tf_op jit(solution)/shard_map/all_gather | solution.py:47
  9.1 269.2 %reduce-scatter.3.cloned.1.call-start = ((), (), s32[]{:S(2)}) async-start(), calls=%async_computation.6 | async-start | bytes 6291456 | tf_op jit(solution)/shard_map/reduce_scatter | solution.py:28
  262.3 157.0 %reduce-scatter.5.cloned.1.call-start = ((), (), s32[]{:S(2)}) async-start(), calls=%async_computation.7 | async-start | bytes 2162688 | tf_op jit(solution)/shard_map/reduce_scatter | solution.py:28
Sparse Core Ops, SparseCore 0:
  9.5 159.5 all-gather.2
  171.2 76.5 all-gather.4
  262.5 15.7 reduce-scatter.2
  281.0 138.3 reduce-scatter.4
where the time goes:
time: 428 us; the launch traced here: 427 us
  waiting for transfers between devices  318 us (74%)
  blocking collectives  70.8 us (17%)
  local copies, waits for them, and re-layouts  19.7 us (5%)
  between operations  13.2 us (3%)
    all_gather x1, waiting for transfers between devices, per_device(): whole = lax.all_gather(tokens, TENSOR, axis=1, tiled=True)  160 us
    reduce_scatter x2, waiting for transfers between devices, reduced_to_own(): pieces = lax.psum_scatter(pieces, axes[k], scatter_dimension=0, tiled=True)  157 us
    all_to_all x1, blocking collectives, per_device(): lax.all_to_all(whole, 'dp', split_axis=1, concat_axis=0, tiled=True)  41.2 us
    all_to_all x1, blocking collectives, summed_on_arrival(): lax.all_to_all(pieces, axis, split_axis=0, concat_axis=0, tiled=True)  29.6 us
  transfers between devices with their start and end apart: 4, of which 3 were waited for; matrix products, arithmetic and copies ran while one was open for 3% of the time, Pallas kernels for 0%

commit v1 on v0

v1 whole, which is shorter than its diff:
```python
import functools

import jax
import jax.numpy as jnp
from jax import lax
from jax.experimental import pallas as pl
from jax.experimental.pallas import tpu as pltpu
from jax.sharding import Mesh
from jax.sharding import PartitionSpec as P

Z = ("zo", "zi")
TENSOR = ("zo", "zi", "core")
F32 = jnp.float32
BF16 = jnp.bfloat16

WINDOW = (-4, -3, -2, -1, 0, 1, 2, 3)


def shifted(array, by):
    n = lax.axis_size(Z)
    return lax.ppermute(array, Z, [(i, (i + by) % n) for i in range(n)])


def swapped(array):
    return lax.ppermute(array, "core", [(0, 1), (1, 0)])


def vmem_call(kernel, outs, *args, flops):
    size = sum(a.size * a.dtype.itemsize for a in (*args, *jax.tree.leaves(outs)))
    return pl.pallas_call(
        kernel,
        out_shape=outs,
        in_specs=[pl.BlockSpec(memory_space=pltpu.VMEM)] * len(args),
        out_specs=jax.tree.map(lambda _: pl.BlockSpec(memory_space=pltpu.VMEM), outs),
        compiler_params=pltpu.CompilerParams(vmem_limit_bytes=40 * 2**20),
        cost_estimate=pl.CostEstimate(flops=flops, bytes_accessed=size, transcendentals=0),
    )(*args)


def up_kernel(mine_refs, theirs_ref, weight_ref, out_ref, rest_ref, total):
    zi, core = lax.axis_index("zi"), lax.axis_index("core")
    n = lax.axis_size("zi")
    width = theirs_ref.shape[2]
    total[...] = jnp.zeros_like(total)
    for i, offset in enumerate(WINDOW):
        residue = lax.rem(zi + (offset + n), n)
        for ref, c in ((mine_refs[i], core), (theirs_ref.at[i], 1 - core)):
            rows = pl.ds(pl.multiple_of((2 * residue + c) * width, width), width)
            total[...] += jnp.dot(ref[...], weight_ref[rows, :], preferred_element_type=F32)
    columns = total.shape[1]
    row = lax.broadcasted_iota(jnp.int32, (columns, columns), 0)
    col = lax.broadcasted_iota(jnp.int32, (columns, columns), 1)
    half = columns // 2
    source = jnp.where(col < half, 2 * col, 2 * (col - half) + 1)
    pick = (row == source).astype(BF16)
    out_ref[...] = jnp.dot(total[...].astype(BF16), pick, preferred_element_type=F32).astype(BF16)
    rows = rest_ref.shape[0]
    stay = total[pl.ds(pl.multiple_of(lax.axis_index("dp") * rows, rows), rows), :]
    rest = (stay - stay.astype(BF16).astype(F32)).astype(BF16)
    rest_ref[...] = jnp.dot(rest, pick, preferred_element_type=F32).astype(BF16)


def hidden_kernel(parts_ref, rest_ref, out_ref):
    total = parts_ref[0].astype(F32) + rest_ref[...].astype(F32)
    for k in range(1, parts_ref.shape[0]):
        total += parts_ref[k].astype(F32)
    half = total.shape[1] // 2
    gate, up = total[:, :half], total[:, half:]
    out_ref[...] = (gate / (1.0 + jnp.exp(-gate)) * up).astype(BF16)


def down_kernel(hidden_ref, other_hidden_ref, weight_ref, other_weight_ref, *out_refs):
    zi, core = lax.axis_index("zi"), lax.axis_index("core")
    n = lax.axis_size("zi")
    width = out_refs[0].shape[1]
    for ref, offset in zip(out_refs, WINDOW):
        residue = lax.rem(zi + (offset + n), n)
        cols = pl.ds(pl.multiple_of((2 * residue + core) * width, width), width)
        term = jnp.dot(hidden_ref[...], weight_ref[:, cols], preferred_element_type=F32)
        term += jnp.dot(other_hidden_ref[...], other_weight_ref[:, cols], preferred_element_type=F32)
        ref[...] = term.astype(ref.dtype)


def per_device(tokens, gate_up_weight, down_weight):
    rows, width = tokens.shape
    dp = lax.axis_size("dp")
    other_weight = swapped(down_weight)
    copies = jnp.broadcast_to(tokens[None], (dp, rows, width))
    copies = lax.all_to_all(copies, "zo", split_axis=0, concat_axis=0, tiled=True)
    block = lax.all_to_all(copies, "dp", split_axis=0, concat_axis=0, tiled=True)
    block = block.reshape(dp * rows, width)
    near = {0: block}
    for s in (2, 1):
        near[-s] = shifted(block, s)
        near[s] = shifted(block, -s)
    near = lax.optimization_barrier(near)
    near[-3] = shifted(near[-2], 1)
    near[-4] = shifted(near[-2], 2)
    near[3] = shifted(near[2], -1)
    mine = [near[o] for o in WINDOW]
    theirs = swapped(jnp.stack(mine))
    columns = gate_up_weight.shape[1]

    def up(*refs):
        up_kernel(refs[: len(WINDOW)], *refs[len(WINDOW) :])

    size = sum(a.size for a in mine) * 4 + gate_up_weight.size * 2
    partial_value, rest = pl.pallas_call(
        up,
        out_shape=(
            jax.ShapeDtypeStruct((dp * rows, columns), BF16),
            jax.ShapeDtypeStruct((rows, columns), BF16),
        ),
        in_specs=[pl.BlockSpec(memory_space=pltpu.VMEM)] * (len(WINDOW) + 2),
        out_specs=(pl.BlockSpec(memory_space=pltpu.VMEM),) * 2,
        scratch_shapes=[pltpu.VMEM((dp * rows, columns), F32)],
        compiler_params=pltpu.CompilerParams(vmem_limit_bytes=40 * 2**20),
        cost_estimate=pl.CostEstimate(
            flops=2 * dp * rows * gate_up_weight.size, bytes_accessed=size, transcendentals=0
        ),
    )(*mine, theirs, gate_up_weight)

    parts = lax.all_to_all(partial_value.reshape(dp, rows, columns), "dp", split_axis=0, concat_axis=0, tiled=True)
    own_hidden = vmem_call(
        hidden_kernel, jax.ShapeDtypeStruct((rows, columns // 2), BF16), parts, rest, flops=10 * parts.size
    )
    hidden = jnp.broadcast_to(own_hidden[None], (dp, *own_hidden.shape))
    hidden = lax.all_to_all(hidden, "dp", split_axis=0, concat_axis=0, tiled=True)
    hidden = hidden.reshape(dp * rows, columns // 2)
    other_hidden = swapped(hidden)

    piece = (dp * rows, width)
    own = vmem_call(
        down_kernel,
        tuple(jax.ShapeDtypeStruct(piece, F32 if o in (-2, 0, 2) else BF16) for o in WINDOW),
        hidden,
        other_hidden,
        down_weight,
        other_weight,
        flops=4 * dp * rows * down_weight.size,
    )
    own = dict(zip(WINDOW, own))
    a2 = shifted(own[-4], -2)
    a1 = shifted(own[-3], -1)
    a3 = shifted(own[3], 1)
    b1 = shifted(own[-1], -1)
    b2 = shifted(own[1], 1)
    b3 = shifted((own[-2] + a1.astype(F32) + a2.astype(F32)).astype(BF16), -2)
    b4 = shifted((own[2] + a3.astype(F32)).astype(BF16), 2)
    window = own[0] + b1.astype(F32) + b2.astype(F32) + b3.astype(F32) + b4.astype(F32)
    out = lax.all_to_all(window.astype(BF16).reshape(dp, rows, width), "dp", split_axis=0, concat_axis=0, tiled=True)
    out = lax.all_to_all(out, "zo", split_axis=0, concat_axis=0, tiled=True)
    return out.astype(F32).sum(axis=0).astype(BF16)


def solution(mesh):
    dp, tensor = mesh.shape["dp"], mesh.shape["tensor"]
    split = Mesh(
        mesh.devices.reshape(mesh.shape["groups"], dp, dp, tensor // (2 * dp), 2),
        ("groups", "dp", *TENSOR),
    )
    placed = (P(("groups", "dp"), TENSOR), P("dp", TENSOR), P(TENSOR, "dp"))
    return jax.shard_map(
        per_device,
        mesh=split,
        in_specs=placed,
        out_specs=P(("groups", "dp"), TENSOR),
        check_vma=False,
    )
```

time: 428 us -> 226 us (0.53)
  the two profiles are of different devices: /device:TPU:34 before, /device:TPU:96 now
where the time goes in v1:
time: 226 us; the launch traced here: 225 us
  blocking collectives  138 us (61%)
  starting transfers between devices  59.8 us (26%)
  waiting for transfers between devices  21 us (9%)
  Pallas kernels  4.04 us (2%)
    all_to_all x1, blocking collectives, per_device(): lax.all_to_all(copies, 'zo', split_axis=0, concat_axis=0, tiled=True)  65.1 us
    ppermute x14, starting transfers between devices, shifted(): return lax.ppermute(array, Z, [(i, (i + by) % n) for i in range(n)])  53.4 us
    all_to_all x1, blocking collectives, per_device(): out = lax.all_to_all(out, 'zo', split_axis=0, concat_axis=0, tiled=True)  32.6 us
    ppermute x14, waiting for transfers between devices, shifted(): return lax.ppermute(array, Z, [(i, (i + by) % n) for i in range(n)])  19.3 us
    all_to_all x1, blocking collectives, per_device(): lax.all_to_all(partial_value.reshape(dp, rows, columns), 'dp', split_axis...  12.6 us
    all_to_all x1, blocking collectives, per_device(): lax.all_to_all(copies, 'dp', split_axis=0, concat_axis=0, tiled=True)  10.3 us
    all_to_all x1, blocking collectives, per_device(): lax.all_to_all(hidden, 'dp', split_axis=0, concat_axis=0, tiled=True)  9.1 us
    all_to_all x1, blocking collectives, per_device(): lax.all_to_all(window.astype(BF16).reshape(dp, rows, width), 'dp', split_...  8.39 us
  transfers between devices with their start and end apart: 17, of which 9 were waited for; matrix products, arithmetic and copies ran while one was open for 0% of the time, Pallas kernels for 1%

profile of v1, /device:TPU:96, one launch (start us, length us, event | category | flops | bytes accessed | tf_op | source)
XLA Modules:
  0.0 225.2 jit_solution(3903184223906114289)
XLA Ops:
  0.0 0.0 copy-start
  0.0 0.9 broadcast_in_dim.4
  0.9 65.1 %all_to_all.30 = bf16[4,128,128]{2,1,0:T(8,128)(2,1)S(1)} all-to-all(bf16[4,128,128]{2,1,0:T(8,128)(2,1)S(1)} %broadcast_in_dim.4), channel_id=1, replica_groups=mesh['groups'=2,'dp'=4,'zo'=4,'zi'=8,'core'=2] {'zo'}, dimensions={0} | all-to-all | bytes 262144 | tf_op jit(solution)/shard_map/all_to_all | solution.py:89
  66.0 10.3 %all_to_all.31 = bf16[4,128,128]{2,1,0:T(8,128)(2,1)S(1)} all-to-all(bf16[4,128,128]{2,1,0:T(8,128)(2,1)S(1)} %all_to_all.30), channel_id=1, replica_groups=mesh['groups'=2,'dp'=4,'zo'=4,'zi'=8,'core'=2] {'dp'}, dimensions={0} | all-to-all | bytes 262144 | tf_op jit(solution)/shard_map/all_to_all | solution.py:90
  76.4 11.6 %collective-permute-start.3 = (bf16[512,128]{1,0:T(8,128)(2,1)S(1)}, bf16[512,128]{1,0:T(8,128)(2,1)S(1)}, u32[]{:S(2)}, u32[]{:S(2)}) collective-permute-start(bf16[512,128]{1,0:T(8,128)(2,1)S(1)} %bitcast.20), channel_id=1, source_target_pairs={{0,60},{2,62},{4,0},{6,2},{8,4},{10,6},{12,8},{14,10},{16,12},{18,... | collective-permute-start | bytes 393224 | tf_op jit(solution)/shard_map/ppermute | solution.py:21
  88.0 2.0 collective-permute-start.2
  89.9 4.0 %collective-permute-start.1 = (bf16[512,128]{1,0:T(8,128)(2,1)S(1)}, bf16[512,128]{1,0:T(8,128)(2,1)S(1)}, u32[]{:S(2)}, u32[]{:S(2)}) collective-permute-start(bf16[512,128]{1,0:T(8,128)(2,1)S(1)} %bitcast.22), channel_id=1, source_target_pairs={{0,2},{2,4},{4,6},{6,8},{8,10},{10,12},{12,14},{14,16},{16,18},{18... | collective-permute-start | bytes 393224 | tf_op jit(solution)/shard_map/ppermute | solution.py:21
  93.9 2.0 collective-permute-start
  95.9 0.0 collective-permute-done.3.refs_6_
  95.9 0.0 collective-permute-done.2.refs_5_
  95.9 2.0 collective-permute-done.1.refs_3_
  97.9 6.5 %collective-permute-done.refs_2_ = bf16[512,128]{1,0:T(8,128)(2,1)S(1)} collective-permute-done((bf16[512,128]{1,0:T(8,128)(2,1)S(1)}, bf16[512,128]{1,0:T(8,128)(2,1)S(1)}, u32[]{:S(2)}, u32[]{:S(2)}) %collective-permute-start) | collective-permute-done | bytes 131104 | tf_op jit(solution)/shard_map/ppermute | solution.py:21
  104.4 1.9 collective-permute-start.4
  106.3 2.0 collective-permute-start.5
  108.3 4.0 %collective-permute-start.6 = (bf16[512,128]{1,0:T(8,128)(2,1)S(1)}, bf16[512,128]{1,0:T(8,128)(2,1)S(1)}, u32[]{:S(2)}, u32[]{:S(2)}) collective-permute-start(bf16[512,128]{1,0:T(8,128)(2,1)S(1)} %collective-permute-done.3.refs_6_), channel_id=1, source_target_pairs={{0,62},{2,0},{4,2},{6,4},{8,6},{10,8},{12,10},{14,12},{16,14},{18,... | collective-permute-start | bytes 393224 | tf_op jit(solution)/shard_map/ppermute | solution.py:21
  112.2 2.1 collective-permute-done.4.refs_0_
  114.4 0.2 collective-permute-done.5.refs_1_
  114.8 0.4 collective-permute-done.6.refs_7_
  115.2 2.0 collective-permute-start.7
  117.1 2.4 %collective-permute-start.9 = (bf16[256,2048]{1,0:T(8,128)(2,1)}, bf16[256,2048]{1,0:T(8,128)(2,1)S(1)}, u32[]{:S(2)}, u32[]{:S(2)}) collective-permute-start(bf16[256,2048]{1,0:T(8,128)(2,1)} %weight_ref.1), channel_id=1, source_target_pairs={{0,1},{1,0},{2,3},{3,2},{4,5},{5,4},{6,7},{7,6},{8,9},{9,8},{10,11... | collective-permute-start | bytes 3145736 | tf_op jit(solution)/shard_map/ppermute | solution.py:25
  119.6 0.2 collective-permute-done.7.refs_8_
  119.8 0.0 copy-done
  119.8 2.7 %shard_map.37 = (bf16[512,512]{1,0:T(8,128)(2,1)S(1)}, bf16[128,512]{1,0:T(8,128)(2,1)S(1)}) custom-call(bf16[512,128]{1,0:T(8,128)(2,1)S(1)} %collective-permute-done.4.refs_0_, bf16[512,128]{1,0:T(8,128)(2,1)S(1)} %collective-permute-done.5.refs_1_, bf16[512,128]{1,0:T(8,128)(2,1)S(1)} %collective-permute-done.refs_2_, ...), custom_call_target="tpu_custom_call" | custom-call | flops 1073741824 | bytes 4194304 | tf_op jit(solution)/shard_map/pallas_call | solution.py:108
  122.4 0.0 copy-start.1
  122.4 12.6 %all_to_all.32.parts_ref = bf16[4,128,512]{2,1,0:T(8,128)(2,1)S(1)} all-to-all(bf16[4,128,512]{2,1,0:T(8,128)(2,1)S(1)} %bitcast.26), channel_id=1, replica_groups=mesh['groups'=2,'dp'=4,'zo'=4,'zi'=8,'core'=2] {'dp'}, dimensions={0} | all-to-all | bytes 1048576 | tf_op jit(solution)/shard_map/all_to_all | solution.py:123
  135.1 0.1 shard_map.38
  135.2 9.1 %all_to_all.33 = bf16[4,128,256]{2,1,0:T(8,128)(2,1)S(1)} all-to-all(bf16[4,128,256]{2,1,0:T(8,128)(2,1)S(1)} %broadcast_in_dim.5), channel_id=1, replica_groups=mesh['groups'=2,'dp'=4,'zo'=4,'zi'=8,'core'=2] {'dp'}, dimensions={0} | all-to-all | bytes 524288 | tf_op jit(solution)/shard_map/all_to_all | solution.py:128
  144.3 1.9 collective-permute-start.8
  146.3 0.0 collective-permute-done.9.other_weight_ref
  146.3 1.5 collective-permute-done.8.other_hidden_ref
  147.8 0.0 copy-done.1
  147.8 1.3 shard_map.39
  149.0 4.2 %collective-permute-start.12 = (bf16[512,128]{1,0:T(8,128)(2,1)S(1)}, bf16[512,128]{1,0:T(8,128)(2,1)S(1)}, u32[]{:S(2)}, u32[]{:S(2)}) collective-permute-start(bf16[512,128]{1,0:T(8,128)(2,1)S(1)} %get-tuple-element.31), channel_id=1, source_target_pairs={{0,62},{2,0},{4,2},{6,4},{8,6},{10,8},{12,10},{14,12},{16,14},{18,... | collective-permute-start | bytes 393224 | tf_op jit(solution)/shard_map/ppermute | solution.py:21
  153.2 5.8 %collective-permute-start.13 = (bf16[512,128]{1,0:T(8,128)(2,1)S(1)}, bf16[512,128]{1,0:T(8,128)(2,1)S(1)}, u32[]{:S(2)}, u32[]{:S(2)}) collective-permute-start(bf16[512,128]{1,0:T(8,128)(2,1)S(1)} %get-tuple-element.32), channel_id=1, source_target_pairs={{0,60},{2,62},{4,0},{6,2},{8,4},{10,6},{12,8},{14,10},{16,12},{18,... | collective-permute-start | bytes 393224 | tf_op jit(solution)/shard_map/ppermute | solution.py:21
  159.1 2.0 collective-permute-start.10
  161.0 4.0 %collective-permute-start.11 = (bf16[512,128]{1,0:T(8,128)(2,1)S(1)}, bf16[512,128]{1,0:T(8,128)(2,1)S(1)}, u32[]{:S(2)}, u32[]{:S(2)}) collective-permute-start(bf16[512,128]{1,0:T(8,128)(2,1)S(1)} %get-tuple-element.29), channel_id=1, source_target_pairs={{0,2},{2,4},{4,6},{6,8},{8,10},{10,12},{12,14},{14,16},{16,18},{18... | collective-permute-start | bytes 393224 | tf_op jit(solution)/shard_map/ppermute | solution.py:21
  165.0 3.2 %collective-permute-start.15 = (bf16[512,128]{1,0:T(8,128)(2,1)S(1)}, bf16[512,128]{1,0:T(8,128)(2,1)S(1)}, u32[]{:S(2)}, u32[]{:S(2)}) collective-permute-start(bf16[512,128]{1,0:T(8,128)(2,1)S(1)} %get-tuple-element.34), channel_id=1, source_target_pairs={{0,2},{2,4},{4,6},{6,8},{8,10},{10,12},{12,14},{14,16},{16,18},{18... | collective-permute-start | bytes 393224 | tf_op jit(solution)/shard_map/ppermute | solution.py:21
  168.1 0.0 collective-permute-done.12
  168.2 0.0 collective-permute-done.13
  168.2 4.0 %collective-permute-start.14 = (bf16[512,128]{1,0:T(8,128)(2,1)S(1)}, bf16[512,128]{1,0:T(8,128)(2,1)S(1)}, u32[]{:S(2)}, u32[]{:S(2)}) collective-permute-start(bf16[512,128]{1,0:T(8,128)(2,1)S(1)} %add_convert_fusion.2), channel_id=1, source_target_pairs={{0,60},{2,62},{4,0},{6,2},{8,4},{10,6},{12,8},{14,10},{16,12},{18,... | collective-permute-start | bytes 393224 | tf_op jit(solution)/shard_map/ppermute | solution.py:21
  172.2 0.0 collective-permute-done.15
  172.3 3.1 %collective-permute-start.16 = (bf16[512,128]{1,0:T(8,128)(2,1)S(1)}, bf16[512,128]{1,0:T(8,128)(2,1)S(1)}, u32[]{:S(2)}, u32[]{:S(2)}) collective-permute-start(bf16[512,128]{1,0:T(8,128)(2,1)S(1)} %add_convert_fusion.1), channel_id=1, source_target_pairs={{0,4},{2,6},{4,8},{6,10},{8,12},{10,14},{12,16},{14,18},{16,20},{1... | collective-permute-start | bytes 393224 | tf_op jit(solution)/shard_map/ppermute | solution.py:21
  175.4 0.0 collective-permute-done.10
  175.4 0.0 collective-permute-done.11
  175.4 2.5 %collective-permute-done.14 = bf16[512,128]{1,0:T(8,128)(2,1)S(1)} collective-permute-done((bf16[512,128]{1,0:T(8,128)(2,1)S(1)}, bf16[512,128]{1,0:T(8,128)(2,1)S(1)}, u32[]{:S(2)}, u32[]{:S(2)}) %collective-permute-start.14) | collective-permute-done | bytes 131104 | tf_op jit(solution)/shard_map/ppermute | solution.py:21
  177.9 5.6 %collective-permute-done.16 = bf16[512,128]{1,0:T(8,128)(2,1)S(1)} collective-permute-done((bf16[512,128]{1,0:T(8,128)(2,1)S(1)}, bf16[512,128]{1,0:T(8,128)(2,1)S(1)}, u32[]{:S(2)}, u32[]{:S(2)}) %collective-permute-start.16) | collective-permute-done | bytes 131104 | tf_op jit(solution)/shard_map/ppermute | solution.py:21
  183.5 0.1 add_convert_fusion
  183.6 8.4 %all_to_all.34 = bf16[4,128,128]{2,1,0:T(8,128)(2,1)S(1)} all-to-all(bf16[4,128,128]{2,1,0:T(8,128)(2,1)S(1)} %bitcast.29), channel_id=1, replica_groups=mesh['groups'=2,'dp'=4,'zo'=4,'zi'=8,'core'=2] {'dp'}, dimensions={0} | all-to-all | bytes 262144 | tf_op jit(solution)/shard_map/all_to_all | solution.py:151
  192.0 32.6 %all_to_all.35 = bf16[4,128,128]{2,1,0:T(8,128)(2,1)S(1)} all-to-all(bf16[4,128,128]{2,1,0:T(8,128)(2,1)S(1)} %all_to_all.34), channel_id=1, replica_groups=mesh['groups'=2,'dp'=4,'zo'=4,'zi'=8,'core'=2] {'zo'}, dimensions={0} | all-to-all | bytes 262144 | tf_op jit(solution)/shard_map/all_to_all | solution.py:152
  224.5 0.6 reduce_sum.12
  (11 shorter events, 0.2 us)
Async XLA Ops:
  0.0 119.8 %copy-start = (bf16[2048,512]{1,0:T(8,128)(2,1)S(1)}, bf16[2048,512]{1,0:T(8,128)(2,1)}, u32[]{:S(2)}) copy-start(bf16[2048,512]{1,0:T(8,128)(2,1)} %refs_9_.1) | copy-start | bytes 6291460
  76.4 19.5 %collective-permute-start.3 = (bf16[512,128]{1,0:T(8,128)(2,1)S(1)}, bf16[512,128]{1,0:T(8,128)(2,1)S(1)}, u32[]{:S(2)}, u32[]{:S(2)}) collective-permute-start(bf16[512,128]{1,0:T(8,128)(2,1)S(1)} %bitcast.20), channel_id=1, source_target_pairs={{0,60},{2,62},{4,0},{6,2},{8,4},{10,6},{12,8},{14,10},{16,12},{18,... | collective-permute-start | bytes 393224 | tf_op jit(solution)/shard_map/ppermute | solution.py:21
  88.0 7.9 %collective-permute-start.2 = (bf16[512,128]{1,0:T(8,128)(2,1)S(1)}, bf16[512,128]{1,0:T(8,128)(2,1)S(1)}, u32[]{:S(2)}, u32[]{:S(2)}) collective-permute-start(bf16[512,128]{1,0:T(8,128)(2,1)S(1)} %bitcast.21), channel_id=1, source_target_pairs={{0,62},{2,0},{4,2},{6,4},{8,6},{10,8},{12,10},{14,12},{16,14},{18,... | collective-permute-start | bytes 393224 | tf_op jit(solution)/shard_map/ppermute | solution.py:21
  89.9 8.0 %collective-permute-start.1 = (bf16[512,128]{1,0:T(8,128)(2,1)S(1)}, bf16[512,128]{1,0:T(8,128)(2,1)S(1)}, u32[]{:S(2)}, u32[]{:S(2)}) collective-permute-start(bf16[512,128]{1,0:T(8,128)(2,1)S(1)} %bitcast.22), channel_id=1, source_target_pairs={{0,2},{2,4},{4,6},{6,8},{8,10},{10,12},{12,14},{14,16},{16,18},{18... | collective-permute-start | bytes 393224 | tf_op jit(solution)/shard_map/ppermute | solution.py:21
  93.9 10.5 %collective-permute-start = (bf16[512,128]{1,0:T(8,128)(2,1)S(1)}, bf16[512,128]{1,0:T(8,128)(2,1)S(1)}, u32[]{:S(2)}, u32[]{:S(2)}) collective-permute-start(bf16[512,128]{1,0:T(8,128)(2,1)S(1)} %bitcast.23), channel_id=1, source_target_pairs={{0,4},{2,6},{4,8},{6,10},{8,12},{10,14},{12,16},{14,18},{16,20},{1... | collective-permute-start | bytes 393224 | tf_op jit(solution)/shard_map/ppermute | solution.py:21
  104.4 10.0 %collective-permute-start.4 = (bf16[512,128]{1,0:T(8,128)(2,1)S(1)}, bf16[512,128]{1,0:T(8,128)(2,1)S(1)}, u32[]{:S(2)}, u32[]{:S(2)}) collective-permute-start(bf16[512,128]{1,0:T(8,128)(2,1)S(1)} %collective-permute-done.refs_2_), channel_id=1, source_target_pairs={{0,4},{2,6},{4,8},{6,10},{8,12},{10,14},{12,16},{14,18},{16,20},{1... | collective-permute-start | bytes 393224 | tf_op jit(solution)/shard_map/ppermute | solution.py:21
  106.3 8.3 %collective-permute-start.5 = (bf16[512,128]{1,0:T(8,128)(2,1)S(1)}, bf16[512,128]{1,0:T(8,128)(2,1)S(1)}, u32[]{:S(2)}, u32[]{:S(2)}) collective-permute-start(bf16[512,128]{1,0:T(8,128)(2,1)S(1)} %collective-permute-done.refs_2_), channel_id=1, source_target_pairs={{0,2},{2,4},{4,6},{6,8},{8,10},{10,12},{12,14},{14,16},{16,18},{18... | collective-permute-start | bytes 393224 | tf_op jit(solution)/shard_map/ppermute | solution.py:21
  108.3 6.9 %collective-permute-start.6 = (bf16[512,128]{1,0:T(8,128)(2,1)S(1)}, bf16[512,128]{1,0:T(8,128)(2,1)S(1)}, u32[]{:S(2)}, u32[]{:S(2)}) collective-permute-start(bf16[512,128]{1,0:T(8,128)(2,1)S(1)} %collective-permute-done.3.refs_6_), channel_id=1, source_target_pairs={{0,62},{2,0},{4,2},{6,4},{8,6},{10,8},{12,10},{14,12},{16,14},{18,... | collective-permute-start | bytes 393224 | tf_op jit(solution)/shard_map/ppermute | solution.py:21
  115.2 4.6 %collective-permute-start.7 = (bf16[8,512,128]{2,1,0:T(8,128)(2,1)S(1)}, bf16[8,512,128]{2,1,0:T(8,128)(2,1)S(1)}, u32[]{:S(2)}, u32[]{:S(2)}) collective-permute-start(bf16[8,512,128]{2,1,0:T(8,128)(2,1)S(1)} %bitcast_dynamic-update-slice_fusion), channel_id=1, source_target_pairs={{0,1},{1,0},{2,3},{3,2},{4,5},{5,4},{6,7},{7,6},{8,9},{9,8},{10,11... | collective-permute-start | bytes 3145736 | tf_op jit(solution)/shard_map/ppermute | solution.py:25
  117.1 29.1 %collective-permute-start.9 = (bf16[256,2048]{1,0:T(8,128)(2,1)}, bf16[256,2048]{1,0:T(8,128)(2,1)S(1)}, u32[]{:S(2)}, u32[]{:S(2)}) collective-permute-start(bf16[256,2048]{1,0:T(8,128)(2,1)} %weight_ref.1), channel_id=1, source_target_pairs={{0,1},{1,0},{2,3},{3,2},{4,5},{5,4},{6,7},{7,6},{8,9},{9,8},{10,11... | collective-permute-start | bytes 3145736 | tf_op jit(solution)/shard_map/ppermute | solution.py:25
  122.4 25.3 %copy-start.1 = (bf16[256,2048]{1,0:T(8,128)(2,1)S(1)}, bf16[256,2048]{1,0:T(8,128)(2,1)}, u32[]{:S(2)}) copy-start(bf16[256,2048]{1,0:T(8,128)(2,1)} %weight_ref.1) | copy-start | bytes 3145732
  144.3 3.4 %collective-permute-start.8 = (bf16[512,256]{1,0:T(8,128)(2,1)S(1)}, bf16[512,256]{1,0:T(8,128)(2,1)S(1)}, u32[]{:S(2)}, u32[]{:S(2)}) collective-permute-start(bf16[512,256]{1,0:T(8,128)(2,1)S(1)} %bitcast.27), channel_id=1, source_target_pairs={{0,1},{1,0},{2,3},{3,2},{4,5},{5,4},{6,7},{7,6},{8,9},{9,8},{10,11... | collective-permute-start | bytes 786440 | tf_op jit(solution)/shard_map/ppermute | solution.py:25
  149.0 19.1 %collective-permute-start.12 = (bf16[512,128]{1,0:T(8,128)(2,1)S(1)}, bf16[512,128]{1,0:T(8,128)(2,1)S(1)}, u32[]{:S(2)}, u32[]{:S(2)}) collective-permute-start(bf16[512,128]{1,0:T(8,128)(2,1)S(1)} %get-tuple-element.31), channel_id=1, source_target_pairs={{0,62},{2,0},{4,2},{6,4},{8,6},{10,8},{12,10},{14,12},{16,14},{18,... | collective-permute-start | bytes 393224 | tf_op jit(solution)/shard_map/ppermute | solution.py:21
  153.2 15.0 %collective-permute-start.13 = (bf16[512,128]{1,0:T(8,128)(2,1)S(1)}, bf16[512,128]{1,0:T(8,128)(2,1)S(1)}, u32[]{:S(2)}, u32[]{:S(2)}) collective-permute-start(bf16[512,128]{1,0:T(8,128)(2,1)S(1)} %get-tuple-element.32), channel_id=1, source_target_pairs={{0,60},{2,62},{4,0},{6,2},{8,4},{10,6},{12,8},{14,10},{16,12},{18,... | collective-permute-start | bytes 393224 | tf_op jit(solution)/shard_map/ppermute | solution.py:21
  159.1 16.3 %collective-permute-start.10 = (bf16[512,128]{1,0:T(8,128)(2,1)S(1)}, bf16[512,128]{1,0:T(8,128)(2,1)S(1)}, u32[]{:S(2)}, u32[]{:S(2)}) collective-permute-start(bf16[512,128]{1,0:T(8,128)(2,1)S(1)} %get-tuple-element.28), channel_id=1, source_target_pairs={{0,62},{2,0},{4,2},{6,4},{8,6},{10,8},{12,10},{14,12},{16,14},{18,... | collective-permute-start | bytes 393224 | tf_op jit(solution)/shard_map/ppermute | solution.py:21
  161.0 14.4 %collective-permute-start.11 = (bf16[512,128]{1,0:T(8,128)(2,1)S(1)}, bf16[512,128]{1,0:T(8,128)(2,1)S(1)}, u32[]{:S(2)}, u32[]{:S(2)}) collective-permute-start(bf16[512,128]{1,0:T(8,128)(2,1)S(1)} %get-tuple-element.29), channel_id=1, source_target_pairs={{0,2},{2,4},{4,6},{6,8},{8,10},{10,12},{12,14},{14,16},{16,18},{18... | collective-permute-start | bytes 393224 | tf_op jit(solution)/shard_map/ppermute | solution.py:21
  165.0 7.2 %collective-permute-start.15 = (bf16[512,128]{1,0:T(8,128)(2,1)S(1)}, bf16[512,128]{1,0:T(8,128)(2,1)S(1)}, u32[]{:S(2)}, u32[]{:S(2)}) collective-permute-start(bf16[512,128]{1,0:T(8,128)(2,1)S(1)} %get-tuple-element.34), channel_id=1, source_target_pairs={{0,2},{2,4},{4,6},{6,8},{8,10},{10,12},{12,14},{14,16},{16,18},{18... | collective-permute-start | bytes 393224 | tf_op jit(solution)/shard_map/ppermute | solution.py:21
  168.2 9.7 %collective-permute-start.14 = (bf16[512,128]{1,0:T(8,128)(2,1)S(1)}, bf16[512,128]{1,0:T(8,128)(2,1)S(1)}, u32[]{:S(2)}, u32[]{:S(2)}) collective-permute-start(bf16[512,128]{1,0:T(8,128)(2,1)S(1)} %add_convert_fusion.2), channel_id=1, source_target_pairs={{0,60},{2,62},{4,0},{6,2},{8,4},{10,6},{12,8},{14,10},{16,12},{18,... | collective-permute-start | bytes 393224 | tf_op jit(solution)/shard_map/ppermute | solution.py:21
  172.3 11.2 %collective-permute-start.16 = (bf16[512,128]{1,0:T(8,128)(2,1)S(1)}, bf16[512,128]{1,0:T(8,128)(2,1)S(1)}, u32[]{:S(2)}, u32[]{:S(2)}) collective-permute-start(bf16[512,128]{1,0:T(8,128)(2,1)S(1)} %add_convert_fusion.1), channel_id=1, source_target_pairs={{0,4},{2,6},{4,8},{6,10},{8,12},{10,14},{12,16},{14,18},{16,20},{1... | collective-permute-start | bytes 393224 | tf_op jit(solution)/shard_map/ppermute | solution.py:21

commit v2 on v1

v2 whole, which is shorter than its diff:
```python
import jax
import jax.numpy as jnp
from jax import lax
from jax.experimental import pallas as pl
from jax.experimental.pallas import tpu as pltpu
from jax.sharding import Mesh
from jax.sharding import PartitionSpec as P

Z = ("zo", "zi")
TENSOR = ("zo", "zi", "core")
F32 = jnp.float32
BF16 = jnp.bfloat16

STEPS = (1, 2, 3, 4)


def shifted(array, by, cores=(0, 1)):
    n = lax.axis_size(Z)
    pairs = [(2 * i + c, 2 * ((i + (by, -by)[c]) % n) + c) for i in range(n) for c in cores]
    return lax.ppermute(array, TENSOR, pairs)


def residue_at(step, core):
    n = lax.axis_size("zi")
    return lax.rem(lax.axis_index("zi") + jnp.where(core == 0, n - step, step), n)


def whole(start, size):
    return pl.ds(pl.multiple_of(start, size), size)


def swapped(array):
    return lax.ppermute(array, "core", [(0, 1), (1, 0)])


def vmem_call(kernel, outs, *args, flops, scratch=()):
    size = sum(a.size * a.dtype.itemsize for a in (*args, *jax.tree.leaves(outs)))
    return pl.pallas_call(
        kernel,
        out_shape=outs,
        in_specs=[pl.BlockSpec(memory_space=pltpu.VMEM)] * len(args),
        out_specs=jax.tree.map(lambda _: pl.BlockSpec(memory_space=pltpu.VMEM), outs),
        scratch_shapes=scratch,
        compiler_params=pltpu.CompilerParams(vmem_limit_bytes=40 * 2**20),
        cost_estimate=pl.CostEstimate(flops=flops, bytes_accessed=size, transcendentals=0),
    )(*args)


def product(pair_ref, weight_ref, residue):
    pair = jnp.concatenate([pair_ref[0], pair_ref[1]], axis=1)
    width = pair.shape[1]
    return jnp.dot(pair, weight_ref[whole(residue * width, width), :], preferred_element_type=F32)


def near_kernel(own_ref, *refs):
    side_refs, weight_ref, total_ref = refs[:-2], refs[-2], refs[-1]
    core = lax.axis_index("core")
    total_ref[...] = product(own_ref, weight_ref, lax.axis_index("zi"))
    for step, ref in zip(STEPS, side_refs):
        total_ref[...] += product(ref, weight_ref, residue_at(step, core))


def up_kernel(total_in_ref, theirs_ref, weight_ref, out_ref, rest_ref, total):
    core = lax.axis_index("core")
    total[...] = total_in_ref[...]
    for k, step in enumerate(STEPS):
        total[...] += product(theirs_ref.at[k], weight_ref, residue_at(step, 1 - core))
    columns = total.shape[1]
    row = lax.broadcasted_iota(jnp.int32, (columns, columns), 0)
    col = lax.broadcasted_iota(jnp.int32, (columns, columns), 1)
    half = columns // 2
    pick = (row == jnp.where(col < half, 2 * col, 2 * (col - half) + 1)).astype(BF16)
    out_ref[...] = jnp.dot(total[...].astype(BF16), pick, preferred_element_type=F32).astype(BF16)
    rows = rest_ref.shape[0]
    stay = total[whole(lax.axis_index("dp") * rows, rows), :]
    rest = (stay - stay.astype(BF16).astype(F32)).astype(BF16)
    rest_ref[...] = jnp.dot(rest, pick, preferred_element_type=F32).astype(BF16)


def hidden_kernel(parts_ref, rest_ref, out_ref):
    total = parts_ref[0].astype(F32) + rest_ref[...].astype(F32)
    for k in range(1, parts_ref.shape[0]):
        total += parts_ref[k].astype(F32)
    half = total.shape[1] // 2
    gate, up = total[:, :half], total[:, half:]
    out_ref[...] = (gate / (1.0 + jnp.exp(-gate)) * up).astype(BF16)


def down_kernel(hidden_ref, weight_ref, other_weight_ref, four_ref, three_ref, one_ref, two_ref, own_ref):
    core = lax.axis_index("core")
    mine, theirs = hidden_ref.at[core], hidden_ref.at[1 - core]

    def term(start, width):
        cols = pl.ds(pl.multiple_of(start, 128), width)
        out = jnp.dot(mine[...], weight_ref[:, cols], preferred_element_type=F32)
        return out + jnp.dot(theirs[...], other_weight_ref[:, cols], preferred_element_type=F32)

    width = four_ref.shape[1]
    for step, ref in zip(STEPS, (one_ref, two_ref, three_ref, four_ref)):
        ref[...] = term(residue_at(step, core) * width, width).astype(ref.dtype)
    half = own_ref.shape[1]
    own_ref[...] = term(lax.axis_index("zi") * width + core * half, half)


def give_kernel(one_ref, two_ref, out_ref):
    width = out_ref.shape[1]
    cols = whole((1 - lax.axis_index("core")) * width, width)
    out_ref[...] = one_ref[:, cols].astype(F32) + two_ref[:, cols].astype(F32)


def window_kernel(own_ref, one_ref, two_ref, given_ref, out_ref):
    core = lax.axis_index("core")
    width = own_ref.shape[1]
    cols = whole(core * width, width)
    total = own_ref[...] + one_ref[:, cols].astype(F32) + two_ref[:, cols].astype(F32)
    out_ref[...] = (total + given_ref[1 - core]).astype(BF16)


def per_device(tokens, gate_up_weight, down_weight):
    rows, width = tokens.shape
    columns = gate_up_weight.shape[1]
    dp = lax.axis_size("dp")
    shape = jax.ShapeDtypeStruct
    other_weight = swapped(down_weight)
    copies = jnp.broadcast_to(tokens[None], (dp, rows, width))
    copies = lax.all_to_all(copies, "zo", split_axis=0, concat_axis=0, tiled=True)
    block = lax.all_to_all(copies, "dp", split_axis=0, concat_axis=0, tiled=True)
    pair = lax.all_gather(block.reshape(dp * rows, width), "core", axis=0)
    two = shifted(pair, 2)
    one = shifted(pair, 1)
    four = shifted(two, 2, cores=(1,))
    three = shifted(two, 1)
    side = (one, two, three, four)
    theirs = swapped(jnp.stack(side))
    total = vmem_call(
        near_kernel,
        shape((dp * rows, columns), F32),
        pair,
        *side,
        gate_up_weight,
        flops=dp * rows * gate_up_weight.size,
    )
    partial_value, rest = vmem_call(
        up_kernel,
        (shape((dp * rows, columns), BF16), shape((rows, columns), BF16)),
        total,
        theirs,
        gate_up_weight,
        flops=dp * rows * gate_up_weight.size,
        scratch=[pltpu.VMEM((dp * rows, columns), F32)],
    )
    parts = partial_value.reshape(dp, rows, columns)
    parts = lax.all_to_all(parts, "dp", split_axis=0, concat_axis=0, tiled=True)
    own_hidden = vmem_call(
        hidden_kernel, shape((rows, columns // 2), BF16), parts, rest, flops=10 * parts.size
    )
    hidden = jnp.broadcast_to(own_hidden[None], (dp, *own_hidden.shape))
    hidden = lax.all_to_all(hidden, "dp", split_axis=0, concat_axis=0, tiled=True)
    hidden = lax.all_gather(hidden.reshape(dp * rows, columns // 2), "core", axis=0)

    block = (dp * rows, 2 * width)
    four, three, one, two, own = vmem_call(
        down_kernel,
        (shape(block, BF16),) * 3 + (shape(block, F32), shape((dp * rows, width), F32)),
        hidden,
        down_weight,
        other_weight,
        flops=4 * dp * rows * down_weight.size,
    )
    four = shifted(four, -2, cores=(1,))
    three = shifted(three, -1)
    one = shifted(one, -1)
    two = shifted((two + three.astype(F32) + four.astype(F32)).astype(BF16), -2)
    given = vmem_call(give_kernel, shape((dp * rows, width), F32), one, two, flops=2 * own.size)
    given = lax.all_gather(given, "core", axis=0)
    out = vmem_call(window_kernel, shape((dp * rows, width), BF16), own, one, two, given, flops=4 * own.size)
    out = out.reshape(dp, rows, width)
    out = lax.all_to_all(out, "dp", split_axis=0, concat_axis=0, tiled=True)
    out = lax.all_to_all(out, "zo", split_axis=0, concat_axis=0, tiled=True)
    return out.astype(F32).sum(axis=0).astype(BF16)


def solution(mesh):
    dp, tensor = mesh.shape["dp"], mesh.shape["tensor"]
    split = Mesh(
        mesh.devices.reshape(mesh.shape["groups"], dp, dp, tensor // (2 * dp), 2),
        ("groups", "dp", *TENSOR),
    )
    placed = (P(("groups", "dp"), TENSOR), P("dp", TENSOR), P(TENSOR, "dp"))
    return jax.shard_map(
        per_device,
        mesh=split,
        in_specs=placed,
        out_specs=P(("groups", "dp"), TENSOR),
        check_vma=False,
    )
```

time: 226 us -> 214 us (0.947)
  the two profiles are of different devices: /device:TPU:96 before, /device:TPU:104 now
where the time goes in v2:
time: 214 us
  blocking collectives  153 us (71%)
  starting transfers between devices  37.3 us (17%)
  waiting for transfers between devices  18.3 us (9%)
  Pallas kernels  2.99 us (1%)
    all_to_all x1, blocking collectives, per_device(): lax.all_to_all(copies, 'zo', split_axis=0, concat_axis=0, tiled=True)  65.2 us
    all_to_all x1, blocking collectives, per_device(): out = lax.all_to_all(out, 'zo', split_axis=0, concat_axis=0, tiled=True)  39.8 us
    ppermute x8, starting transfers between devices, shifted(): return lax.ppermute(array, TENSOR, pairs)  31.5 us
    ppermute x8, waiting for transfers between devices, shifted(): return lax.ppermute(array, TENSOR, pairs)  18.3 us
    all_to_all x1, blocking collectives, per_device(): parts = lax.all_to_all(parts, 'dp', split_axis=0, concat_axis=0, tiled=True)  12.8 us
    all_to_all x1, blocking collectives, per_device(): lax.all_to_all(copies, 'dp', split_axis=0, concat_axis=0, tiled=True)  10.3 us
    all_to_all x1, blocking collectives, per_device(): lax.all_to_all(hidden, 'dp', split_axis=0, concat_axis=0, tiled=True)  9.1 us
    all_to_all x1, blocking collectives, per_device(): out = lax.all_to_all(out, 'dp', split_axis=0, concat_axis=0, tiled=True)  8.5 us
  transfers between devices with their start and end apart: 10, of which 3 were waited for; matrix products, arithmetic and copies ran while one was open for 0% of the time, Pallas kernels for 1%

profile of v2, /device:TPU:104, one launch (start us, length us, event | category | flops | bytes accessed | tf_op | source)
XLA Modules:
  0.0 213.8 jit_solution(14987242754475742579)
XLA Ops:
  0.0 0.0 copy-start.1
  0.0 0.0 copy-start
  0.0 0.9 broadcast_in_dim.4
  0.9 65.2 %all_to_all.30 = bf16[4,128,128]{2,1,0:T(8,128)(2,1)S(1)} all-to-all(bf16[4,128,128]{2,1,0:T(8,128)(2,1)S(1)} %broadcast_in_dim.4), channel_id=1, replica_groups=mesh['groups'=2,'dp'=4,'zo'=4,'zi'=8,'core'=2] {'zo'}, dimensions={0} | all-to-all | bytes 262144 | tf_op jit(solution)/shard_map/all_to_all | solution.py:126
  66.2 10.3 %all_to_all.31 = bf16[4,128,128]{2,1,0:T(8,128)(2,1)S(1)} all-to-all(bf16[4,128,128]{2,1,0:T(8,128)(2,1)S(1)} %all_to_all.30), channel_id=1, replica_groups=mesh['groups'=2,'dp'=4,'zo'=4,'zi'=8,'core'=2] {'dp'}, dimensions={0} | all-to-all | bytes 262144 | tf_op jit(solution)/shard_map/all_to_all | solution.py:127
  76.5 2.0 all_gather.12.own_ref
  78.5 5.2 %collective-permute-start.1 = (bf16[2,512,128]{2,1,0:T(8,128)(2,1)S(1)}, bf16[2,512,128]{2,1,0:T(8,128)(2,1)S(1)}, u32[]{:S(2)}, u32[]{:S(2)}) collective-permute-start(bf16[2,512,128]{2,1,0:T(8,128)(2,1)S(1)} %all_gather.12.own_ref), channel_id=1, source_target_pairs={{0,4},{1,61},{2,6},{3,63},{4,8},{5,1},{6,10},{7,3},{8,12},{9,5},{1... | collective-permute-start | bytes 786440 | tf_op jit(solution)/shard_map/ppermute | solution.py:20
  83.8 6.7 %collective-permute-start = (bf16[2,512,128]{2,1,0:T(8,128)(2,1)S(1)}, bf16[2,512,128]{2,1,0:T(8,128)(2,1)S(1)}, u32[]{:S(2)}, u32[]{:S(2)}) collective-permute-start(bf16[2,512,128]{2,1,0:T(8,128)(2,1)S(1)} %all_gather.12.own_ref), channel_id=1, source_target_pairs={{0,2},{1,63},{2,4},{3,1},{4,6},{5,3},{6,8},{7,5},{8,10},{9,7},{10,... | collective-permute-start | bytes 786440 | tf_op jit(solution)/shard_map/ppermute | solution.py:20
  90.5 6.8 %collective-permute-done.1.refs_1_ = bf16[2,512,128]{2,1,0:T(8,128)(2,1)S(1)} collective-permute-done((bf16[2,512,128]{2,1,0:T(8,128)(2,1)S(1)}, bf16[2,512,128]{2,1,0:T(8,128)(2,1)S(1)}, u32[]{:S(2)}, u32[]{:S(2)}) %collective-permute-start.1) | collective-permute-done | bytes 262176 | tf_op jit(solution)/shard_map/ppermute | solution.py:20
  97.3 0.7 collective-permute-start.3
  97.9 2.0 collective-permute-start.2
  99.9 0.0 collective-permute-done.refs_0_
  99.9 0.0 collective-permute-done.3.refs_3_
  99.9 6.3 %collective-permute-done.2.refs_2_ = bf16[2,512,128]{2,1,0:T(8,128)(2,1)S(1)} collective-permute-done((bf16[2,512,128]{2,1,0:T(8,128)(2,1)S(1)}, bf16[2,512,128]{2,1,0:T(8,128)(2,1)S(1)}, u32[]{:S(2)}, u32[]{:S(2)}) %collective-permute-start.2) | collective-permute-done | bytes 262176 | tf_op jit(solution)/shard_map/ppermute | solution.py:20
  106.2 0.1 pad_maximum_fusion
  106.4 3.9 %collective-permute-start.4 = (bf16[4,2,512,128]{3,2,1,0:T(8,128)(2,1)S(1)}, bf16[4,2,512,128]{3,2,1,0:T(8,128)(2,1)S(1)}, u32[]{:S(2)}, u32[]{:S(2)}) collective-permute-start(bf16[4,2,512,128]{3,2,1,0:T(8,128)(2,1)S(1)} %pad_maximum_fusion), channel_id=1, source_target_pairs={{0,1},{1,0},{2,3},{3,2},{4,5},{5,4},{6,7},{7,6},{8,9},{9,8},{10,11... | collective-permute-start | bytes 3145736 | tf_op jit(solution)/shard_map/ppermute | solution.py:33
  110.3 0.0 copy-done.1
  110.3 2.0 collective-permute-start.5
  112.2 0.0 copy-done
  112.2 0.9 shard_map.37.total_in_ref
  113.1 0.0 collective-permute-done.4.theirs_ref
  113.1 1.1 shard_map.38
  114.2 12.8 %all_to_all.32.parts_ref = bf16[4,128,512]{2,1,0:T(8,128)(2,1)S(1)} all-to-all(bf16[4,128,512]{2,1,0:T(8,128)(2,1)S(1)} %bitcast.14), channel_id=1, replica_groups=mesh['groups'=2,'dp'=4,'zo'=4,'zi'=8,'core'=2] {'dp'}, dimensions={0} | all-to-all | bytes 1048576 | tf_op jit(solution)/shard_map/all_to_all | solution.py:153
  127.0 0.1 shard_map.39
  127.2 9.1 %all_to_all.33 = bf16[4,128,256]{2,1,0:T(8,128)(2,1)S(1)} all-to-all(bf16[4,128,256]{2,1,0:T(8,128)(2,1)S(1)} %broadcast_in_dim.5), channel_id=1, replica_groups=mesh['groups'=2,'dp'=4,'zo'=4,'zi'=8,'core'=2] {'dp'}, dimensions={0} | all-to-all | bytes 524288 | tf_op jit(solution)/shard_map/all_to_all | solution.py:158
  136.3 2.2 %all_gather.13.hidden_ref = bf16[2,512,256]{2,1,0:T(8,128)(2,1)S(1)} all-gather(bf16[1,512,256]{2,1,0:T(8,128)(2,1)S(1)} %bitcast.16), channel_id=1, replica_groups=mesh['groups'=2,'dp'=4,'zo'=4,'zi'=8,'core'=2] {'core'}, dimensions={0}, use_global_device_ids=true | all-gather | bytes 786432 | tf_op jit(solution)/shard_map/all_gather | solution.py:159
  138.5 0.0 collective-permute-done.5.other_weight_ref
  138.5 0.9 shard_map.40
  139.3 4.7 %collective-permute-start.7 = (bf16[512,256]{1,0:T(8,128)(2,1)S(1)}, bf16[512,256]{1,0:T(8,128)(2,1)S(1)}, u32[]{:S(2)}, u32[]{:S(2)}) collective-permute-start(bf16[512,256]{1,0:T(8,128)(2,1)S(1)} %get-tuple-element.17), channel_id=1, source_target_pairs={{0,62},{1,3},{2,0},{3,5},{4,2},{5,7},{6,4},{7,9},{8,6},{9,11},{10,... | collective-permute-start | bytes 786440 | tf_op jit(solution)/shard_map/ppermute | solution.py:20
  144.0 0.7 collective-permute-start.8
  144.7 5.3 %collective-permute-start.6 = (bf16[512,256]{1,0:T(8,128)(2,1)S(1)}, bf16[512,256]{1,0:T(8,128)(2,1)S(1)}, u32[]{:S(2)}, u32[]{:S(2)}) collective-permute-start(bf16[512,256]{1,0:T(8,128)(2,1)S(1)} %get-tuple-element.15), channel_id=1, source_target_pairs={{0,62},{1,3},{2,0},{3,5},{4,2},{5,7},{6,4},{7,9},{8,6},{9,11},{10,... | collective-permute-start | bytes 786440 | tf_op jit(solution)/shard_map/ppermute | solution.py:20
  150.0 0.0 collective-permute-done.7
  150.1 0.0 collective-permute-done.8
  150.1 0.1 add_convert_fusion
  150.2 6.3 %collective-permute-start.9 = (bf16[512,256]{1,0:T(8,128)(2,1)S(1)}, bf16[512,256]{1,0:T(8,128)(2,1)S(1)}, u32[]{:S(2)}, u32[]{:S(2)}) collective-permute-start(bf16[512,256]{1,0:T(8,128)(2,1)S(1)} %add_convert_fusion), channel_id=1, source_target_pairs={{0,60},{1,5},{2,62},{3,7},{4,0},{5,9},{6,2},{7,11},{8,4},{9,13},{1... | collective-permute-start | bytes 786440 | tf_op jit(solution)/shard_map/ppermute | solution.py:20
  156.4 0.0 collective-permute-done.6.one_ref
  156.5 5.2 %collective-permute-done.9.two_ref = bf16[512,256]{1,0:T(8,128)(2,1)S(1)} collective-permute-done((bf16[512,256]{1,0:T(8,128)(2,1)S(1)}, bf16[512,256]{1,0:T(8,128)(2,1)S(1)}, u32[]{:S(2)}, u32[]{:S(2)}) %collective-permute-start.9) | collective-permute-done | bytes 262176 | tf_op jit(solution)/shard_map/ppermute | solution.py:20
  161.7 3.1 %all-gather = f32[1024,128]{1,0:T(8,128)S(1)} all-gather(f32[512,128]{1,0:T(8,128)S(1)} %shard_map.41), channel_id=2, replica_groups=mesh['groups'=2,'dp'=4,'zo'=4,'zi'=8,'core'=2] {'core'}, dimensions={0}, use_global_device_ids=true | all-gather | bytes 786432 | tf_op jit(solution)/shard_map/all_gather | solution.py:175
  164.8 0.1 shard_map.42
  164.8 8.5 %all_to_all.34 = bf16[4,128,128]{2,1,0:T(8,128)(2,1)S(1)} all-to-all(bf16[4,128,128]{2,1,0:T(8,128)(2,1)S(1)} %bitcast.15), channel_id=1, replica_groups=mesh['groups'=2,'dp'=4,'zo'=4,'zi'=8,'core'=2] {'dp'}, dimensions={0} | all-to-all | bytes 262144 | tf_op jit(solution)/shard_map/all_to_all | solution.py:178
  173.3 39.8 %all_to_all.35 = bf16[4,128,128]{2,1,0:T(8,128)(2,1)S(1)} all-to-all(bf16[4,128,128]{2,1,0:T(8,128)(2,1)S(1)} %all_to_all.34), channel_id=1, replica_groups=mesh['groups'=2,'dp'=4,'zo'=4,'zi'=8,'core'=2] {'zo'}, dimensions={0} | all-to-all | bytes 262144 | tf_op jit(solution)/shard_map/all_to_all | solution.py:179
  213.2 0.6 reduce_sum.12
  (2 shorter events, 0.0 us)
Async XLA Ops:
  0.0 110.3 %copy-start.1 = (bf16[256,2048]{1,0:T(8,128)(2,1)S(1)}, bf16[256,2048]{1,0:T(8,128)(2,1)}, u32[]{:S(2)}) copy-start(bf16[256,2048]{1,0:T(8,128)(2,1)} %weight_ref.3) | copy-start | bytes 3145732
  0.0 112.2 %copy-start = (bf16[2048,512]{1,0:T(8,128)(2,1)S(1)}, bf16[2048,512]{1,0:T(8,128)(2,1)}, u32[]{:S(2)}) copy-start(bf16[2048,512]{1,0:T(8,128)(2,1)} %weight_ref.2) | copy-start | bytes 6291460
  78.5 18.7 %collective-permute-start.1 = (bf16[2,512,128]{2,1,0:T(8,128)(2,1)S(1)}, bf16[2,512,128]{2,1,0:T(8,128)(2,1)S(1)}, u32[]{:S(2)}, u32[]{:S(2)}) collective-permute-start(bf16[2,512,128]{2,1,0:T(8,128)(2,1)S(1)} %all_gather.12.own_ref), channel_id=1, source_target_pairs={{0,4},{1,61},{2,6},{3,63},{4,8},{5,1},{6,10},{7,3},{8,12},{9,5},{1... | collective-permute-start | bytes 786440 | tf_op jit(solution)/shard_map/ppermute | solution.py:20
  83.8 16.1 %collective-permute-start = (bf16[2,512,128]{2,1,0:T(8,128)(2,1)S(1)}, bf16[2,512,128]{2,1,0:T(8,128)(2,1)S(1)}, u32[]{:S(2)}, u32[]{:S(2)}) collective-permute-start(bf16[2,512,128]{2,1,0:T(8,128)(2,1)S(1)} %all_gather.12.own_ref), channel_id=1, source_target_pairs={{0,2},{1,63},{2,4},{3,1},{4,6},{5,3},{6,8},{7,5},{8,10},{9,7},{10,... | collective-permute-start | bytes 786440 | tf_op jit(solution)/shard_map/ppermute | solution.py:20
  97.3 2.6 %collective-permute-start.3 = (bf16[2,512,128]{2,1,0:T(8,128)(2,1)S(1)}, bf16[2,512,128]{2,1,0:T(8,128)(2,1)S(1)}, u32[]{:S(2)}, u32[]{:S(2)}) collective-permute-start(bf16[2,512,128]{2,1,0:T(8,128)(2,1)S(1)} %collective-permute-done.1.refs_1_), channel_id=1, source_target_pairs={{1,61},{3,63},{5,1},{7,3},{9,5},{11,7},{13,9},{15,11},{17,13},{19,... | collective-permute-start | bytes 786440 | tf_op jit(solution)/shard_map/ppermute | solution.py:20
  97.9 8.3 %collective-permute-start.2 = (bf16[2,512,128]{2,1,0:T(8,128)(2,1)S(1)}, bf16[2,512,128]{2,1,0:T(8,128)(2,1)S(1)}, u32[]{:S(2)}, u32[]{:S(2)}) collective-permute-start(bf16[2,512,128]{2,1,0:T(8,128)(2,1)S(1)} %collective-permute-done.1.refs_1_), channel_id=1, source_target_pairs={{0,2},{1,63},{2,4},{3,1},{4,6},{5,3},{6,8},{7,5},{8,10},{9,7},{10,... | collective-permute-start | bytes 786440 | tf_op jit(solution)/shard_map/ppermute | solution.py:20
  106.4 6.7 %collective-permute-start.4 = (bf16[4,2,512,128]{3,2,1,0:T(8,128)(2,1)S(1)}, bf16[4,2,512,128]{3,2,1,0:T(8,128)(2,1)S(1)}, u32[]{:S(2)}, u32[]{:S(2)}) collective-permute-start(bf16[4,2,512,128]{3,2,1,0:T(8,128)(2,1)S(1)} %pad_maximum_fusion), channel_id=1, source_target_pairs={{0,1},{1,0},{2,3},{3,2},{4,5},{5,4},{6,7},{7,6},{8,9},{9,8},{10,11... | collective-permute-start | bytes 3145736 | tf_op jit(solution)/shard_map/ppermute | solution.py:33
  110.3 28.2 %collective-permute-start.5 = (bf16[256,2048]{1,0:T(8,128)(2,1)S(1)}, bf16[256,2048]{1,0:T(8,128)(2,1)S(1)}, u32[]{:S(2)}, u32[]{:S(2)}) collective-permute-start(bf16[256,2048]{1,0:T(8,128)(2,1)S(1)} %copy-done.1), channel_id=1, source_target_pairs={{0,1},{1,0},{2,3},{3,2},{4,5},{5,4},{6,7},{7,6},{8,9},{9,8},{10,11... | collective-permute-start | bytes 3145736 | tf_op jit(solution)/shard_map/ppermute | solution.py:33
  139.3 10.7 %collective-permute-start.7 = (bf16[512,256]{1,0:T(8,128)(2,1)S(1)}, bf16[512,256]{1,0:T(8,128)(2,1)S(1)}, u32[]{:S(2)}, u32[]{:S(2)}) collective-permute-start(bf16[512,256]{1,0:T(8,128)(2,1)S(1)} %get-tuple-element.17), channel_id=1, source_target_pairs={{0,62},{1,3},{2,0},{3,5},{4,2},{5,7},{6,4},{7,9},{8,6},{9,11},{10,... | collective-permute-start | bytes 786440 | tf_op jit(solution)/shard_map/ppermute | solution.py:20
  144.0 6.0 %collective-permute-start.8 = (bf16[512,256]{1,0:T(8,128)(2,1)S(1)}, bf16[512,256]{1,0:T(8,128)(2,1)S(1)}, u32[]{:S(2)}, u32[]{:S(2)}) collective-permute-start(bf16[512,256]{1,0:T(8,128)(2,1)S(1)} %get-tuple-element.18), channel_id=1, source_target_pairs={{1,5},{3,7},{5,9},{7,11},{9,13},{11,15},{13,17},{15,19},{17,21},{1... | collective-permute-start | bytes 786440 | tf_op jit(solution)/shard_map/ppermute | solution.py:20
  144.7 11.7 %collective-permute-start.6 = (bf16[512,256]{1,0:T(8,128)(2,1)S(1)}, bf16[512,256]{1,0:T(8,128)(2,1)S(1)}, u32[]{:S(2)}, u32[]{:S(2)}) collective-permute-start(bf16[512,256]{1,0:T(8,128)(2,1)S(1)} %get-tuple-element.15), channel_id=1, source_target_pairs={{0,62},{1,3},{2,0},{3,5},{4,2},{5,7},{6,4},{7,9},{8,6},{9,11},{10,... | collective-permute-start | bytes 786440 | tf_op jit(solution)/shard_map/ppermute | solution.py:20
  150.2 11.5 %collective-permute-start.9 = (bf16[512,256]{1,0:T(8,128)(2,1)S(1)}, bf16[512,256]{1,0:T(8,128)(2,1)S(1)}, u32[]{:S(2)}, u32[]{:S(2)}) collective-permute-start(bf16[512,256]{1,0:T(8,128)(2,1)S(1)} %add_convert_fusion), channel_id=1, source_target_pairs={{0,60},{1,5},{2,62},{3,7},{4,0},{5,9},{6,2},{7,11},{8,4},{9,13},{1... | collective-permute-start | bytes 786440 | tf_op jit(solution)/shard_map/ppermute | solution.py:20

commit v3 on v2

--- a/solution.py
+++ b/solution.py
@@ -47,7 +47,8 @@
 
 
 def product(pair_ref, weight_ref, residue):
-    pair = jnp.concatenate([pair_ref[0], pair_ref[1]], axis=1)
+    blocks = [jnp.concatenate([pair_ref[k], pair_ref[k + 1]], axis=1) for k in range(0, pair_ref.shape[0], 2)]
+    pair = jnp.concatenate(blocks)
     width = pair.shape[1]
     return jnp.dot(pair, weight_ref[whole(residue * width, width), :], preferred_element_type=F32)
 
@@ -122,10 +123,9 @@
     dp = lax.axis_size("dp")
     shape = jax.ShapeDtypeStruct
     other_weight = swapped(down_weight)
-    copies = jnp.broadcast_to(tokens[None], (dp, rows, width))
-    copies = lax.all_to_all(copies, "zo", split_axis=0, concat_axis=0, tiled=True)
-    block = lax.all_to_all(copies, "dp", split_axis=0, concat_axis=0, tiled=True)
-    pair = lax.all_gather(block.reshape(dp * rows, width), "core", axis=0)
+    copies = lax.all_gather(tokens, "zo", axis=0)
+    copies = jnp.repeat(copies, 2, axis=0)
+    pair = lax.all_to_all(copies, ("dp", "core"), split_axis=0, concat_axis=0, tiled=True)
     two = shifted(pair, 2)
     one = shifted(pair, 1)
     four = shifted(two, 2, cores=(1,))

time: 214 us -> 214 us (level)
  waiting for transfers between devices: 18.3 us -> 23.9 us
  blocking collectives: 153 us -> 150 us
    all_to_all x2 -> x1, blocking collectives: 75.6 us -> 11.9 us  [per_device(): lax.all_to_all(copies, ('dp', 'core'), split_axis=0, concat_axis=0, tiled...]
    all_gather x1, blocking collectives: 2.01 us -> 61.1 us  [per_device(): copies = lax.all_gather(tokens, 'zo', axis=0)]
    ppermute x8, waiting for transfers between devices: 18.3 us -> 23.9 us  [shifted(): return lax.ppermute(array, TENSOR, pairs)]
where the time goes in v3:
time: 214 us; the launch traced here: 213 us
  blocking collectives  150 us (70%)
  starting transfers between devices  35.5 us (17%)
  waiting for transfers between devices  23.9 us (11%)
  Pallas kernels  2.99 us (1%)
    all_gather x1, blocking collectives, per_device(): copies = lax.all_gather(tokens, 'zo', axis=0)  61.1 us
    all_to_all x1, blocking collectives, per_device(): out = lax.all_to_all(out, 'zo', split_axis=0, concat_axis=0, tiled=True)  41.1 us
    ppermute x8, starting transfers between devices, shifted(): return lax.ppermute(array, TENSOR, pairs)  29.7 us
    ppermute x8, waiting for transfers between devices, shifted(): return lax.ppermute(array, TENSOR, pairs)  23.9 us
    all_to_all x1, blocking collectives, per_device(): parts = lax.all_to_all(parts, 'dp', split_axis=0, concat_axis=0, tiled=True)  12.9 us
    all_to_all x1, blocking collectives, per_device(): lax.all_to_all(copies, ('dp', 'core'), split_axis=0, concat_axis=0, tiled...  11.9 us
    all_to_all x1, blocking collectives, per_device(): lax.all_to_all(hidden, 'dp', split_axis=0, concat_axis=0, tiled=True)  9.1 us
    all_to_all x1, blocking collectives, per_device(): out = lax.all_to_all(out, 'dp', split_axis=0, concat_axis=0, tiled=True)  8.5 us
  transfers between devices with their start and end apart: 10, of which 3 were waited for; matrix products, arithmetic and copies ran while one was open for 0% of the time, Pallas kernels for 1%

profile of v3, /device:TPU:104, one launch (start us, length us, event | category | flops | bytes accessed | tf_op | source)
XLA Modules:
  0.0 213.1 jit_solution(16243446887143352748)
XLA Ops:
  0.0 0.0 copy-start.1
  0.0 0.0 copy-start
  0.0 61.1 %all-gather = bf16[512,128]{1,0:T(8,128)(2,1)S(1)} all-gather(bf16[128,128]{1,0:T(8,128)(2,1)} %param.3), channel_id=2, replica_groups=mesh['groups'=2,'dp'=4,'zo'=4,'zi'=8,'core'=2] {'zo'}, dimensions={0}, use_global_device_ids=true | all-gather | bytes 163840 | tf_op jit(solution)/shard_map/all_gather | solution.py:126
  61.2 11.9 %all_to_all.25.own_ref = bf16[8,128,128]{2,1,0:T(8,128)(2,1)S(1)} all-to-all(bf16[8,128,128]{2,1,0:T(8,128)(2,1)S(1)} %bitcast.18), channel_id=1, replica_groups=mesh['groups'=2,'dp'=4,'zo'=4,'zi'=8,'core'=2] {'dp','core'}, dimensions={0} | all-to-all | bytes 524288 | tf_op jit(solution)/shard_map/all_to_all | solution.py:128
  73.1 5.2 %collective-permute-start.1 = (bf16[8,128,128]{2,1,0:T(8,128)(2,1)S(1)}, bf16[8,128,128]{2,1,0:T(8,128)(2,1)S(1)}, u32[]{:S(2)}, u32[]{:S(2)}) collective-permute-start(bf16[8,128,128]{2,1,0:T(8,128)(2,1)S(1)} %all_to_all.25.own_ref), channel_id=1, source_target_pairs={{0,4},{1,61},{2,6},{3,63},{4,8},{5,1},{6,10},{7,3},{8,12},{9,5},{1... | collective-permute-start | bytes 786440 | tf_op jit(solution)/shard_map/ppermute | solution.py:20
  78.3 5.0 %collective-permute-start = (bf16[8,128,128]{2,1,0:T(8,128)(2,1)S(1)}, bf16[8,128,128]{2,1,0:T(8,128)(2,1)S(1)}, u32[]{:S(2)}, u32[]{:S(2)}) collective-permute-start(bf16[8,128,128]{2,1,0:T(8,128)(2,1)S(1)} %all_to_all.25.own_ref), channel_id=1, source_target_pairs={{0,2},{1,63},{2,4},{3,1},{4,6},{5,3},{6,8},{7,5},{8,10},{9,7},{10,... | collective-permute-start | bytes 786440 | tf_op jit(solution)/shard_map/ppermute | solution.py:20
  83.3 12.1 %collective-permute-done.1.refs_1_ = bf16[8,128,128]{2,1,0:T(8,128)(2,1)S(1)} collective-permute-done((bf16[8,128,128]{2,1,0:T(8,128)(2,1)S(1)}, bf16[8,128,128]{2,1,0:T(8,128)(2,1)S(1)}, u32[]{:S(2)}, u32[]{:S(2)}) %collective-permute-start.1) | collective-permute-done | bytes 262176 | tf_op jit(solution)/shard_map/ppermute | solution.py:20
  95.4 0.7 collective-permute-start.3
  96.1 2.0 collective-permute-start.2
  98.1 0.0 collective-permute-done.refs_0_
  98.1 0.0 collective-permute-done.3.refs_3_
  98.1 6.3 %collective-permute-done.2.refs_2_ = bf16[8,128,128]{2,1,0:T(8,128)(2,1)S(1)} collective-permute-done((bf16[8,128,128]{2,1,0:T(8,128)(2,1)S(1)}, bf16[8,128,128]{2,1,0:T(8,128)(2,1)S(1)}, u32[]{:S(2)}, u32[]{:S(2)}) %collective-permute-start.2) | collective-permute-done | bytes 262176 | tf_op jit(solution)/shard_map/ppermute | solution.py:20
  104.4 0.1 pad_maximum_fusion
  104.6 3.9 %collective-permute-start.4 = (bf16[4,8,128,128]{3,2,1,0:T(8,128)(2,1)S(1)}, bf16[4,8,128,128]{3,2,1,0:T(8,128)(2,1)S(1)}, u32[]{:S(2)}, u32[]{:S(2)}) collective-permute-start(bf16[4,8,128,128]{3,2,1,0:T(8,128)(2,1)S(1)} %pad_maximum_fusion), channel_id=1, source_target_pairs={{0,1},{1,0},{2,3},{3,2},{4,5},{5,4},{6,7},{7,6},{8,9},{9,8},{10,11... | collective-permute-start | bytes 3145736 | tf_op jit(solution)/shard_map/ppermute | solution.py:33
  108.5 0.0 copy-done.1
  108.5 2.0 collective-permute-start.5
  110.4 0.0 copy-done
  110.4 0.9 shard_map.37.total_in_ref
  111.3 0.0 collective-permute-done.4.theirs_ref
  111.3 1.1 shard_map.38
  112.4 12.9 %all_to_all.26.parts_ref = bf16[4,128,512]{2,1,0:T(8,128)(2,1)S(1)} all-to-all(bf16[4,128,512]{2,1,0:T(8,128)(2,1)S(1)} %bitcast.15), channel_id=1, replica_groups=mesh['groups'=2,'dp'=4,'zo'=4,'zi'=8,'core'=2] {'dp'}, dimensions={0} | all-to-all | bytes 1048576 | tf_op jit(solution)/shard_map/all_to_all | solution.py:153
  125.2 0.1 shard_map.39
  125.4 9.1 %all_to_all.27 = bf16[4,128,256]{2,1,0:T(8,128)(2,1)S(1)} all-to-all(bf16[4,128,256]{2,1,0:T(8,128)(2,1)S(1)} %broadcast_in_dim.10), channel_id=1, replica_groups=mesh['groups'=2,'dp'=4,'zo'=4,'zi'=8,'core'=2] {'dp'}, dimensions={0} | all-to-all | bytes 524288 | tf_op jit(solution)/shard_map/all_to_all | solution.py:158
  134.5 2.2 %all_gather.17.hidden_ref = bf16[2,512,256]{2,1,0:T(8,128)(2,1)S(1)} all-gather(bf16[1,512,256]{2,1,0:T(8,128)(2,1)S(1)} %bitcast.17), channel_id=1, replica_groups=mesh['groups'=2,'dp'=4,'zo'=4,'zi'=8,'core'=2] {'core'}, dimensions={0}, use_global_device_ids=true | all-gather | bytes 786432 | tf_op jit(solution)/shard_map/all_gather | solution.py:159
  136.7 0.0 collective-permute-done.5.other_weight_ref
  136.7 0.9 shard_map.40
  137.6 4.5 %collective-permute-start.7 = (bf16[512,256]{1,0:T(8,128)(2,1)S(1)}, bf16[512,256]{1,0:T(8,128)(2,1)S(1)}, u32[]{:S(2)}, u32[]{:S(2)}) collective-permute-start(bf16[512,256]{1,0:T(8,128)(2,1)S(1)} %get-tuple-element.17), channel_id=1, source_target_pairs={{0,62},{1,3},{2,0},{3,5},{4,2},{5,7},{6,4},{7,9},{8,6},{9,11},{10,... | collective-permute-start | bytes 786440 | tf_op jit(solution)/shard_map/ppermute | solution.py:20
  142.1 0.7 collective-permute-start.8
  142.8 5.3 %collective-permute-start.6 = (bf16[512,256]{1,0:T(8,128)(2,1)S(1)}, bf16[512,256]{1,0:T(8,128)(2,1)S(1)}, u32[]{:S(2)}, u32[]{:S(2)}) collective-permute-start(bf16[512,256]{1,0:T(8,128)(2,1)S(1)} %get-tuple-element.15), channel_id=1, source_target_pairs={{0,62},{1,3},{2,0},{3,5},{4,2},{5,7},{6,4},{7,9},{8,6},{9,11},{10,... | collective-permute-start | bytes 786440 | tf_op jit(solution)/shard_map/ppermute | solution.py:20
  148.1 0.0 collective-permute-done.7
  148.1 0.0 collective-permute-done.8
  148.2 0.1 add_convert_fusion
  148.2 6.3 %collective-permute-start.9 = (bf16[512,256]{1,0:T(8,128)(2,1)S(1)}, bf16[512,256]{1,0:T(8,128)(2,1)S(1)}, u32[]{:S(2)}, u32[]{:S(2)}) collective-permute-start(bf16[512,256]{1,0:T(8,128)(2,1)S(1)} %add_convert_fusion), channel_id=1, source_target_pairs={{0,60},{1,5},{2,62},{3,7},{4,0},{5,9},{6,2},{7,11},{8,4},{9,13},{1... | collective-permute-start | bytes 786440 | tf_op jit(solution)/shard_map/ppermute | solution.py:20
  154.5 0.0 collective-permute-done.6.one_ref
  154.5 5.4 %collective-permute-done.9.two_ref = bf16[512,256]{1,0:T(8,128)(2,1)S(1)} collective-permute-done((bf16[512,256]{1,0:T(8,128)(2,1)S(1)}, bf16[512,256]{1,0:T(8,128)(2,1)S(1)}, u32[]{:S(2)}, u32[]{:S(2)}) %collective-permute-start.9) | collective-permute-done | bytes 262176 | tf_op jit(solution)/shard_map/ppermute | solution.py:20
  160.0 2.9 %all-gather.1 = f32[1024,128]{1,0:T(8,128)S(1)} all-gather(f32[512,128]{1,0:T(8,128)S(1)} %shard_map.41), channel_id=3, replica_groups=mesh['groups'=2,'dp'=4,'zo'=4,'zi'=8,'core'=2] {'core'}, dimensions={0}, use_global_device_ids=true | all-gather | bytes 786432 | tf_op jit(solution)/shard_map/all_gather | solution.py:175
  162.9 0.1 shard_map.42
  162.9 8.5 %all_to_all.28 = bf16[4,128,128]{2,1,0:T(8,128)(2,1)S(1)} all-to-all(bf16[4,128,128]{2,1,0:T(8,128)(2,1)S(1)} %bitcast.16), channel_id=1, replica_groups=mesh['groups'=2,'dp'=4,'zo'=4,'zi'=8,'core'=2] {'dp'}, dimensions={0} | all-to-all | bytes 262144 | tf_op jit(solution)/shard_map/all_to_all | solution.py:178
  171.4 41.1 %all_to_all.29 = bf16[4,128,128]{2,1,0:T(8,128)(2,1)S(1)} all-to-all(bf16[4,128,128]{2,1,0:T(8,128)(2,1)S(1)} %all_to_all.28), channel_id=1, replica_groups=mesh['groups'=2,'dp'=4,'zo'=4,'zi'=8,'core'=2] {'zo'}, dimensions={0} | all-to-all | bytes 262144 | tf_op jit(solution)/shard_map/all_to_all | solution.py:179
  212.5 0.6 reduce_sum.12
  (3 shorter events, 0.1 us)
Async XLA Ops:
  0.0 108.5 %copy-start.1 = (bf16[256,2048]{1,0:T(8,128)(2,1)S(1)}, bf16[256,2048]{1,0:T(8,128)(2,1)}, u32[]{:S(2)}) copy-start(bf16[256,2048]{1,0:T(8,128)(2,1)} %weight_ref.3) | copy-start | bytes 3145732
  0.0 110.4 %copy-start = (bf16[2048,512]{1,0:T(8,128)(2,1)S(1)}, bf16[2048,512]{1,0:T(8,128)(2,1)}, u32[]{:S(2)}) copy-start(bf16[2048,512]{1,0:T(8,128)(2,1)} %weight_ref.2) | copy-start | bytes 6291460
  73.1 22.4 %collective-permute-start.1 = (bf16[8,128,128]{2,1,0:T(8,128)(2,1)S(1)}, bf16[8,128,128]{2,1,0:T(8,128)(2,1)S(1)}, u32[]{:S(2)}, u32[]{:S(2)}) collective-permute-start(bf16[8,128,128]{2,1,0:T(8,128)(2,1)S(1)} %all_to_all.25.own_ref), channel_id=1, source_target_pairs={{0,4},{1,61},{2,6},{3,63},{4,8},{5,1},{6,10},{7,3},{8,12},{9,5},{1... | collective-permute-start | bytes 786440 | tf_op jit(solution)/shard_map/ppermute | solution.py:20
  78.3 19.8 %collective-permute-start = (bf16[8,128,128]{2,1,0:T(8,128)(2,1)S(1)}, bf16[8,128,128]{2,1,0:T(8,128)(2,1)S(1)}, u32[]{:S(2)}, u32[]{:S(2)}) collective-permute-start(bf16[8,128,128]{2,1,0:T(8,128)(2,1)S(1)} %all_to_all.25.own_ref), channel_id=1, source_target_pairs={{0,2},{1,63},{2,4},{3,1},{4,6},{5,3},{6,8},{7,5},{8,10},{9,7},{10,... | collective-permute-start | bytes 786440 | tf_op jit(solution)/shard_map/ppermute | solution.py:20
  95.4 2.6 %collective-permute-start.3 = (bf16[8,128,128]{2,1,0:T(8,128)(2,1)S(1)}, bf16[8,128,128]{2,1,0:T(8,128)(2,1)S(1)}, u32[]{:S(2)}, u32[]{:S(2)}) collective-permute-start(bf16[8,128,128]{2,1,0:T(8,128)(2,1)S(1)} %collective-permute-done.1.refs_1_), channel_id=1, source_target_pairs={{1,61},{3,63},{5,1},{7,3},{9,5},{11,7},{13,9},{15,11},{17,13},{19,... | collective-permute-start | bytes 786440 | tf_op jit(solution)/shard_map/ppermute | solution.py:20
  96.1 8.3 %collective-permute-start.2 = (bf16[8,128,128]{2,1,0:T(8,128)(2,1)S(1)}, bf16[8,128,128]{2,1,0:T(8,128)(2,1)S(1)}, u32[]{:S(2)}, u32[]{:S(2)}) collective-permute-start(bf16[8,128,128]{2,1,0:T(8,128)(2,1)S(1)} %collective-permute-done.1.refs_1_), channel_id=1, source_target_pairs={{0,2},{1,63},{2,4},{3,1},{4,6},{5,3},{6,8},{7,5},{8,10},{9,7},{10,... | collective-permute-start | bytes 786440 | tf_op jit(solution)/shard_map/ppermute | solution.py:20
  104.6 6.7 %collective-permute-start.4 = (bf16[4,8,128,128]{3,2,1,0:T(8,128)(2,1)S(1)}, bf16[4,8,128,128]{3,2,1,0:T(8,128)(2,1)S(1)}, u32[]{:S(2)}, u32[]{:S(2)}) collective-permute-start(bf16[4,8,128,128]{3,2,1,0:T(8,128)(2,1)S(1)} %pad_maximum_fusion), channel_id=1, source_target_pairs={{0,1},{1,0},{2,3},{3,2},{4,5},{5,4},{6,7},{7,6},{8,9},{9,8},{10,11... | collective-permute-start | bytes 3145736 | tf_op jit(solution)/shard_map/ppermute | solution.py:33
  108.5 28.2 %collective-permute-start.5 = (bf16[256,2048]{1,0:T(8,128)(2,1)S(1)}, bf16[256,2048]{1,0:T(8,128)(2,1)S(1)}, u32[]{:S(2)}, u32[]{:S(2)}) collective-permute-start(bf16[256,2048]{1,0:T(8,128)(2,1)S(1)} %copy-done.1), channel_id=1, source_target_pairs={{0,1},{1,0},{2,3},{3,2},{4,5},{5,4},{6,7},{7,6},{8,9},{9,8},{10,11... | collective-permute-start | bytes 3145736 | tf_op jit(solution)/shard_map/ppermute | solution.py:33
  137.6 10.6 %collective-permute-start.7 = (bf16[512,256]{1,0:T(8,128)(2,1)S(1)}, bf16[512,256]{1,0:T(8,128)(2,1)S(1)}, u32[]{:S(2)}, u32[]{:S(2)}) collective-permute-start(bf16[512,256]{1,0:T(8,128)(2,1)S(1)} %get-tuple-element.17), channel_id=1, source_target_pairs={{0,62},{1,3},{2,0},{3,5},{4,2},{5,7},{6,4},{7,9},{8,6},{9,11},{10,... | collective-permute-start | bytes 786440 | tf_op jit(solution)/shard_map/ppermute | solution.py:20
  142.1 6.0 %collective-permute-start.8 = (bf16[512,256]{1,0:T(8,128)(2,1)S(1)}, bf16[512,256]{1,0:T(8,128)(2,1)S(1)}, u32[]{:S(2)}, u32[]{:S(2)}) collective-permute-start(bf16[512,256]{1,0:T(8,128)(2,1)S(1)} %get-tuple-element.18), channel_id=1, source_target_pairs={{1,5},{3,7},{5,9},{7,11},{9,13},{11,15},{13,17},{15,19},{17,21},{1... | collective-permute-start | bytes 786440 | tf_op jit(solution)/shard_map/ppermute | solution.py:20
  142.8 11.7 %collective-permute-start.6 = (bf16[512,256]{1,0:T(8,128)(2,1)S(1)}, bf16[512,256]{1,0:T(8,128)(2,1)S(1)}, u32[]{:S(2)}, u32[]{:S(2)}) collective-permute-start(bf16[512,256]{1,0:T(8,128)(2,1)S(1)} %get-tuple-element.15), channel_id=1, source_target_pairs={{0,62},{1,3},{2,0},{3,5},{4,2},{5,7},{6,4},{7,9},{8,6},{9,11},{10,... | collective-permute-start | bytes 786440 | tf_op jit(solution)/shard_map/ppermute | solution.py:20
  148.2 11.7 %collective-permute-start.9 = (bf16[512,256]{1,0:T(8,128)(2,1)S(1)}, bf16[512,256]{1,0:T(8,128)(2,1)S(1)}, u32[]{:S(2)}, u32[]{:S(2)}) collective-permute-start(bf16[512,256]{1,0:T(8,128)(2,1)S(1)} %add_convert_fusion), channel_id=1, source_target_pairs={{0,60},{1,5},{2,62},{3,7},{4,0},{5,9},{6,2},{7,11},{8,4},{9,13},{1... | collective-permute-start | bytes 786440 | tf_op jit(solution)/shard_map/ppermute | solution.py:20

commit v4 on v3

--- a/solution.py
+++ b/solution.py
@@ -123,11 +123,13 @@
     dp = lax.axis_size("dp")
     shape = jax.ShapeDtypeStruct
     other_weight = swapped(down_weight)
-    copies = lax.all_gather(tokens, "zo", axis=0)
+    copies = jnp.broadcast_to(tokens[None], (dp, rows, width))
+    copies = lax.all_to_all(copies, "zo", split_axis=0, concat_axis=0, tiled=True)
     copies = jnp.repeat(copies, 2, axis=0)
     pair = lax.all_to_all(copies, ("dp", "core"), split_axis=0, concat_axis=0, tiled=True)
     two = shifted(pair, 2)
     one = shifted(pair, 1)
+    two, other_weight = lax.optimization_barrier((two, other_weight))
     four = shifted(two, 2, cores=(1,))
     three = shifted(two, 1)
     side = (one, two, three, four)

time: 214 us -> 213 us (level)
  blocking collectives: 150 us -> 87.2 us
  starting transfers between devices: 35.5 us -> 78.7 us
  waiting for transfers between devices: 23.9 us -> 41 us
    all_gather x1 -> x0, blocking collectives: 61.1 us -> none  [per_device(): copies = lax.all_gather(tokens, 'zo', axis=0)]
    all_to_all x0 -> x1, starting transfers between devices: none -> 42.1 us  [per_device(): lax.all_to_all(copies, 'zo', split_axis=0, concat_axis=0, tiled=True)]
    all_to_all x0 -> x1, waiting for transfers between devices: none -> 21.3 us  [per_device(): lax.all_to_all(copies, 'zo', split_axis=0, concat_axis=0, tiled=True)]
    ppermute x8, waiting for transfers between devices: 23.9 us -> 18.3 us  [shifted(): return lax.ppermute(array, TENSOR, pairs)]
  transfers between devices with their start and end apart: 10 -> 11, of which waited for: 3 -> 5; matrix products, arithmetic and copies ran while one was open for 0% -> 0% of each run, Pallas kernels for 1% -> 0%
where the time goes in v4:
time: 213 us
  blocking collectives  87.2 us (41%)
  starting transfers between devices  78.7 us (37%)
  waiting for transfers between devices  41 us (19%)
  Pallas kernels  2.97 us (1%)
    all_to_all x1, starting transfers between devices, per_device(): lax.all_to_all(copies, 'zo', split_axis=0, concat_axis=0, tiled=True)  42.1 us
    all_to_all x1, blocking collectives, per_device(): out = lax.all_to_all(out, 'zo', split_axis=0, concat_axis=0, tiled=True)  39.6 us
    ppermute x8, starting transfers between devices, shifted(): return lax.ppermute(array, TENSOR, pairs)  31.5 us
    all_to_all x1, waiting for transfers between devices, per_device(): lax.all_to_all(copies, 'zo', split_axis=0, concat_axis=0, tiled=True)  21.3 us
    ppermute x8, waiting for transfers between devices, shifted(): return lax.ppermute(array, TENSOR, pairs)  18.3 us
    all_to_all x1, blocking collectives, per_device(): parts = lax.all_to_all(parts, 'dp', split_axis=0, concat_axis=0, tiled=True)  12.9 us
    all_to_all x1, blocking collectives, per_device(): lax.all_to_all(copies, ('dp', 'core'), split_axis=0, concat_axis=0, tiled...  11.9 us
    all_to_all x1, blocking collectives, per_device(): lax.all_to_all(hidden, 'dp', split_axis=0, concat_axis=0, tiled=True)  9.1 us
  transfers between devices with their start and end apart: 11, of which 5 were waited for; matrix products, arithmetic and copies ran while one was open for 0% of the time, Pallas kernels for 0%

profile of v4, /device:TPU:104, one launch (start us, length us, event | category | flops | bytes accessed | tf_op | source)
XLA Modules:
  0.0 212.6 jit_solution(10845028385288620800)
XLA Ops:
  0.0 0.0 copy-start
  0.0 1.6 broadcast_in_dim.6
  1.6 42.1 %all-to-all-start = ((bf16[4,128,128]{2,1,0:T(8,128)(2,1)}), bf16[4,128,128]{2,1,0:T(8,128)(2,1)S(1)}, u32[]{:S(2)}, u32[]{:S(2)}) async-start(bf16[4,128,128]{2,1,0:T(8,128)(2,1)} %broadcast_in_dim.6), calls=%async_computation | async-start | bytes 262144 | tf_op jit(solution)/shard_map/all_to_all | solution.py:127
  43.7 1.9 collective-permute-start.2
  45.6 21.3 %all-to-all-done = bf16[4,128,128]{2,1,0:T(8,128)(2,1)S(1)} async-done(((bf16[4,128,128]{2,1,0:T(8,128)(2,1)}), bf16[4,128,128]{2,1,0:T(8,128)(2,1)S(1)}, u32[]{:S(2)}, u32[]{:S(2)}) %all-to-all-start) | async-done | bytes 131104 | tf_op jit(solution)/shard_map/all_to_all | solution.py:127
  66.9 11.9 %all_to_all.30.own_ref = bf16[8,128,128]{2,1,0:T(8,128)(2,1)S(1)} all-to-all(bf16[8,128,128]{2,1,0:T(8,128)(2,1)S(1)} %bitcast.17), channel_id=1, replica_groups=mesh['groups'=2,'dp'=4,'zo'=4,'zi'=8,'core'=2] {'dp','core'}, dimensions={0} | all-to-all | bytes 524288 | tf_op jit(solution)/shard_map/all_to_all | solution.py:129
  78.8 5.2 %collective-permute-start.1 = (bf16[8,128,128]{2,1,0:T(8,128)(2,1)S(1)}, bf16[8,128,128]{2,1,0:T(8,128)(2,1)S(1)}, u32[]{:S(2)}, u32[]{:S(2)}) collective-permute-start(bf16[8,128,128]{2,1,0:T(8,128)(2,1)S(1)} %all_to_all.30.own_ref), channel_id=1, source_target_pairs={{0,4},{1,61},{2,6},{3,63},{4,8},{5,1},{6,10},{7,3},{8,12},{9,5},{1... | collective-permute-start | bytes 786440 | tf_op jit(solution)/shard_map/ppermute | solution.py:20
  84.1 6.7 %collective-permute-start = (bf16[8,128,128]{2,1,0:T(8,128)(2,1)S(1)}, bf16[8,128,128]{2,1,0:T(8,128)(2,1)S(1)}, u32[]{:S(2)}, u32[]{:S(2)}) collective-permute-start(bf16[8,128,128]{2,1,0:T(8,128)(2,1)S(1)} %all_to_all.30.own_ref), channel_id=1, source_target_pairs={{0,2},{1,63},{2,4},{3,1},{4,6},{5,3},{6,8},{7,5},{8,10},{9,7},{10,... | collective-permute-start | bytes 786440 | tf_op jit(solution)/shard_map/ppermute | solution.py:20
  90.7 0.0 collective-permute-done.2.other_weight_ref
  90.7 6.8 %collective-permute-done.1.refs_1_ = bf16[8,128,128]{2,1,0:T(8,128)(2,1)S(1)} collective-permute-done((bf16[8,128,128]{2,1,0:T(8,128)(2,1)S(1)}, bf16[8,128,128]{2,1,0:T(8,128)(2,1)S(1)}, u32[]{:S(2)}, u32[]{:S(2)}) %collective-permute-start.1) | collective-permute-done | bytes 262176 | tf_op jit(solution)/shard_map/ppermute | solution.py:20
  97.6 0.7 collective-permute-start.4
  98.2 2.0 collective-permute-start.3
  100.2 0.0 collective-permute-done.refs_0_
  100.2 0.0 collective-permute-done.4.refs_3_
  100.2 6.3 %collective-permute-done.3.refs_2_ = bf16[8,128,128]{2,1,0:T(8,128)(2,1)S(1)} collective-permute-done((bf16[8,128,128]{2,1,0:T(8,128)(2,1)S(1)}, bf16[8,128,128]{2,1,0:T(8,128)(2,1)S(1)}, u32[]{:S(2)}, u32[]{:S(2)}) %collective-permute-start.3) | collective-permute-done | bytes 262176 | tf_op jit(solution)/shard_map/ppermute | solution.py:20
  106.5 0.1 pad_maximum_fusion
  106.7 3.2 %collective-permute-start.5 = (bf16[4,8,128,128]{3,2,1,0:T(8,128)(2,1)S(1)}, bf16[4,8,128,128]{3,2,1,0:T(8,128)(2,1)S(1)}, u32[]{:S(2)}, u32[]{:S(2)}) collective-permute-start(bf16[4,8,128,128]{3,2,1,0:T(8,128)(2,1)S(1)} %pad_maximum_fusion), channel_id=1, source_target_pairs={{0,1},{1,0},{2,3},{3,2},{4,5},{5,4},{6,7},{7,6},{8,9},{9,8},{10,11... | collective-permute-start | bytes 3145736 | tf_op jit(solution)/shard_map/ppermute | solution.py:33
  109.9 0.0 copy-done
  109.9 0.9 shard_map.37.total_in_ref
  110.7 1.4 collective-permute-done.5.theirs_ref
  112.1 1.1 shard_map.38
  113.2 0.0 copy-start.1
  113.2 12.9 %all_to_all.31.parts_ref = bf16[4,128,512]{2,1,0:T(8,128)(2,1)S(1)} all-to-all(bf16[4,128,512]{2,1,0:T(8,128)(2,1)S(1)} %bitcast.14), channel_id=1, replica_groups=mesh['groups'=2,'dp'=4,'zo'=4,'zi'=8,'core'=2] {'dp'}, dimensions={0} | all-to-all | bytes 1048576 | tf_op jit(solution)/shard_map/all_to_all | solution.py:155
  126.1 0.1 shard_map.39
  126.2 9.1 %all_to_all.32 = bf16[4,128,256]{2,1,0:T(8,128)(2,1)S(1)} all-to-all(bf16[4,128,256]{2,1,0:T(8,128)(2,1)S(1)} %broadcast_in_dim.8), channel_id=1, replica_groups=mesh['groups'=2,'dp'=4,'zo'=4,'zi'=8,'core'=2] {'dp'}, dimensions={0} | all-to-all | bytes 524288 | tf_op jit(solution)/shard_map/all_to_all | solution.py:160
  135.3 2.2 %all_gather.9.hidden_ref = bf16[2,512,256]{2,1,0:T(8,128)(2,1)S(1)} all-gather(bf16[1,512,256]{2,1,0:T(8,128)(2,1)S(1)} %bitcast.16), channel_id=1, replica_groups=mesh['groups'=2,'dp'=4,'zo'=4,'zi'=8,'core'=2] {'core'}, dimensions={0}, use_global_device_ids=true | all-gather | bytes 786432 | tf_op jit(solution)/shard_map/all_gather | solution.py:161
  137.5 0.0 copy-done.1
  137.5 0.9 shard_map.40
  138.4 4.6 %collective-permute-start.7 = (bf16[512,256]{1,0:T(8,128)(2,1)S(1)}, bf16[512,256]{1,0:T(8,128)(2,1)S(1)}, u32[]{:S(2)}, u32[]{:S(2)}) collective-permute-start(bf16[512,256]{1,0:T(8,128)(2,1)S(1)} %get-tuple-element.21), channel_id=1, source_target_pairs={{0,62},{1,3},{2,0},{3,5},{4,2},{5,7},{6,4},{7,9},{8,6},{9,11},{10,... | collective-permute-start | bytes 786440 | tf_op jit(solution)/shard_map/ppermute | solution.py:20
  143.1 0.7 collective-permute-start.8
  143.7 5.3 %collective-permute-start.6 = (bf16[512,256]{1,0:T(8,128)(2,1)S(1)}, bf16[512,256]{1,0:T(8,128)(2,1)S(1)}, u32[]{:S(2)}, u32[]{:S(2)}) collective-permute-start(bf16[512,256]{1,0:T(8,128)(2,1)S(1)} %get-tuple-element.19), channel_id=1, source_target_pairs={{0,62},{1,3},{2,0},{3,5},{4,2},{5,7},{6,4},{7,9},{8,6},{9,11},{10,... | collective-permute-start | bytes 786440 | tf_op jit(solution)/shard_map/ppermute | solution.py:20
  149.1 0.0 collective-permute-done.7
  149.1 0.0 collective-permute-done.8
  149.1 0.1 add_convert_fusion
  149.2 6.3 %collective-permute-start.9 = (bf16[512,256]{1,0:T(8,128)(2,1)S(1)}, bf16[512,256]{1,0:T(8,128)(2,1)S(1)}, u32[]{:S(2)}, u32[]{:S(2)}) collective-permute-start(bf16[512,256]{1,0:T(8,128)(2,1)S(1)} %add_convert_fusion), channel_id=1, source_target_pairs={{0,60},{1,5},{2,62},{3,7},{4,0},{5,9},{6,2},{7,11},{8,4},{9,13},{1... | collective-permute-start | bytes 786440 | tf_op jit(solution)/shard_map/ppermute | solution.py:20
  155.5 0.0 collective-permute-done.6.one_ref
  155.5 5.2 %collective-permute-done.9.two_ref = bf16[512,256]{1,0:T(8,128)(2,1)S(1)} collective-permute-done((bf16[512,256]{1,0:T(8,128)(2,1)S(1)}, bf16[512,256]{1,0:T(8,128)(2,1)S(1)}, u32[]{:S(2)}, u32[]{:S(2)}) %collective-permute-start.9) | collective-permute-done | bytes 262176 | tf_op jit(solution)/shard_map/ppermute | solution.py:20
  160.7 3.1 %all-gather = f32[1024,128]{1,0:T(8,128)S(1)} all-gather(f32[512,128]{1,0:T(8,128)S(1)} %shard_map.41), channel_id=2, replica_groups=mesh['groups'=2,'dp'=4,'zo'=4,'zi'=8,'core'=2] {'core'}, dimensions={0}, use_global_device_ids=true | all-gather | bytes 786432 | tf_op jit(solution)/shard_map/all_gather | solution.py:177
  163.8 0.1 shard_map.42
  163.9 8.5 %all_to_all.33 = bf16[4,128,128]{2,1,0:T(8,128)(2,1)S(1)} all-to-all(bf16[4,128,128]{2,1,0:T(8,128)(2,1)S(1)} %bitcast.15), channel_id=1, replica_groups=mesh['groups'=2,'dp'=4,'zo'=4,'zi'=8,'core'=2] {'dp'}, dimensions={0} | all-to-all | bytes 262144 | tf_op jit(solution)/shard_map/all_to_all | solution.py:180
  172.4 39.6 %all_to_all.34 = bf16[4,128,128]{2,1,0:T(8,128)(2,1)S(1)} all-to-all(bf16[4,128,128]{2,1,0:T(8,128)(2,1)S(1)} %all_to_all.33), channel_id=1, replica_groups=mesh['groups'=2,'dp'=4,'zo'=4,'zi'=8,'core'=2] {'zo'}, dimensions={0} | all-to-all | bytes 262144 | tf_op jit(solution)/shard_map/all_to_all | solution.py:181
  212.0 0.6 reduce_sum.12
  (3 shorter events, 0.1 us)
Async XLA Ops:
  0.0 109.9 %copy-start = (bf16[2048,512]{1,0:T(8,128)(2,1)S(1)}, bf16[2048,512]{1,0:T(8,128)(2,1)}, u32[]{:S(2)}) copy-start(bf16[2048,512]{1,0:T(8,128)(2,1)} %weight_ref.2) | copy-start | bytes 6291460
  1.6 65.3 %all-to-all-start = ((bf16[4,128,128]{2,1,0:T(8,128)(2,1)}), bf16[4,128,128]{2,1,0:T(8,128)(2,1)S(1)}, u32[]{:S(2)}, u32[]{:S(2)}) async-start(bf16[4,128,128]{2,1,0:T(8,128)(2,1)} %broadcast_in_dim.6), calls=%async_computation | async-start | bytes 262144 | tf_op jit(solution)/shard_map/all_to_all | solution.py:127
  43.7 47.1 %collective-permute-start.2 = (bf16[256,2048]{1,0:T(8,128)(2,1)}, bf16[256,2048]{1,0:T(8,128)(2,1)S(1)}, u32[]{:S(2)}, u32[]{:S(2)}) collective-permute-start(bf16[256,2048]{1,0:T(8,128)(2,1)} %weight_ref.3), channel_id=1, source_target_pairs={{0,1},{1,0},{2,3},{3,2},{4,5},{5,4},{6,7},{7,6},{8,9},{9,8},{10,11... | collective-permute-start | bytes 3145736 | tf_op jit(solution)/shard_map/ppermute | solution.py:33
  78.8 18.7 %collective-permute-start.1 = (bf16[8,128,128]{2,1,0:T(8,128)(2,1)S(1)}, bf16[8,128,128]{2,1,0:T(8,128)(2,1)S(1)}, u32[]{:S(2)}, u32[]{:S(2)}) collective-permute-start(bf16[8,128,128]{2,1,0:T(8,128)(2,1)S(1)} %all_to_all.30.own_ref), channel_id=1, source_target_pairs={{0,4},{1,61},{2,6},{3,63},{4,8},{5,1},{6,10},{7,3},{8,12},{9,5},{1... | collective-permute-start | bytes 786440 | tf_op jit(solution)/shard_map/ppermute | solution.py:20
  84.1 16.1 %collective-permute-start = (bf16[8,128,128]{2,1,0:T(8,128)(2,1)S(1)}, bf16[8,128,128]{2,1,0:T(8,128)(2,1)S(1)}, u32[]{:S(2)}, u32[]{:S(2)}) collective-permute-start(bf16[8,128,128]{2,1,0:T(8,128)(2,1)S(1)} %all_to_all.30.own_ref), channel_id=1, source_target_pairs={{0,2},{1,63},{2,4},{3,1},{4,6},{5,3},{6,8},{7,5},{8,10},{9,7},{10,... | collective-permute-start | bytes 786440 | tf_op jit(solution)/shard_map/ppermute | solution.py:20
  97.6 2.6 %collective-permute-start.4 = (bf16[8,128,128]{2,1,0:T(8,128)(2,1)S(1)}, bf16[8,128,128]{2,1,0:T(8,128)(2,1)S(1)}, u32[]{:S(2)}, u32[]{:S(2)}) collective-permute-start(bf16[8,128,128]{2,1,0:T(8,128)(2,1)S(1)} %collective-permute-done.1.refs_1_), channel_id=1, source_target_pairs={{1,61},{3,63},{5,1},{7,3},{9,5},{11,7},{13,9},{15,11},{17,13},{19,... | collective-permute-start | bytes 786440 | tf_op jit(solution)/shard_map/ppermute | solution.py:20
  98.2 8.3 %collective-permute-start.3 = (bf16[8,128,128]{2,1,0:T(8,128)(2,1)S(1)}, bf16[8,128,128]{2,1,0:T(8,128)(2,1)S(1)}, u32[]{:S(2)}, u32[]{:S(2)}) collective-permute-start(bf16[8,128,128]{2,1,0:T(8,128)(2,1)S(1)} %collective-permute-done.1.refs_1_), channel_id=1, source_target_pairs={{0,2},{1,63},{2,4},{3,1},{4,6},{5,3},{6,8},{7,5},{8,10},{9,7},{10,... | collective-permute-start | bytes 786440 | tf_op jit(solution)/shard_map/ppermute | solution.py:20
  106.7 5.5 %collective-permute-start.5 = (bf16[4,8,128,128]{3,2,1,0:T(8,128)(2,1)S(1)}, bf16[4,8,128,128]{3,2,1,0:T(8,128)(2,1)S(1)}, u32[]{:S(2)}, u32[]{:S(2)}) collective-permute-start(bf16[4,8,128,128]{3,2,1,0:T(8,128)(2,1)S(1)} %pad_maximum_fusion), channel_id=1, source_target_pairs={{0,1},{1,0},{2,3},{3,2},{4,5},{5,4},{6,7},{7,6},{8,9},{9,8},{10,11... | collective-permute-start | bytes 3145736 | tf_op jit(solution)/shard_map/ppermute | solution.py:33
  113.2 24.3 %copy-start.1 = (bf16[256,2048]{1,0:T(8,128)(2,1)S(1)}, bf16[256,2048]{1,0:T(8,128)(2,1)}, u32[]{:S(2)}) copy-start(bf16[256,2048]{1,0:T(8,128)(2,1)} %weight_ref.3) | copy-start | bytes 3145732
  138.4 10.7 %collective-permute-start.7 = (bf16[512,256]{1,0:T(8,128)(2,1)S(1)}, bf16[512,256]{1,0:T(8,128)(2,1)S(1)}, u32[]{:S(2)}, u32[]{:S(2)}) collective-permute-start(bf16[512,256]{1,0:T(8,128)(2,1)S(1)} %get-tuple-element.21), channel_id=1, source_target_pairs={{0,62},{1,3},{2,0},{3,5},{4,2},{5,7},{6,4},{7,9},{8,6},{9,11},{10,... | collective-permute-start | bytes 786440 | tf_op jit(solution)/shard_map/ppermute | solution.py:20
  143.1 6.0 %collective-permute-start.8 = (bf16[512,256]{1,0:T(8,128)(2,1)S(1)}, bf16[512,256]{1,0:T(8,128)(2,1)S(1)}, u32[]{:S(2)}, u32[]{:S(2)}) collective-permute-start(bf16[512,256]{1,0:T(8,128)(2,1)S(1)} %get-tuple-element.22), channel_id=1, source_target_pairs={{1,5},{3,7},{5,9},{7,11},{9,13},{11,15},{13,17},{15,19},{17,21},{1... | collective-permute-start | bytes 786440 | tf_op jit(solution)/shard_map/ppermute | solution.py:20
  143.7 11.8 %collective-permute-start.6 = (bf16[512,256]{1,0:T(8,128)(2,1)S(1)}, bf16[512,256]{1,0:T(8,128)(2,1)S(1)}, u32[]{:S(2)}, u32[]{:S(2)}) collective-permute-start(bf16[512,256]{1,0:T(8,128)(2,1)S(1)} %get-tuple-element.19), channel_id=1, source_target_pairs={{0,62},{1,3},{2,0},{3,5},{4,2},{5,7},{6,4},{7,9},{8,6},{9,11},{10,... | collective-permute-start | bytes 786440 | tf_op jit(solution)/shard_map/ppermute | solution.py:20
  149.2 11.5 %collective-permute-start.9 = (bf16[512,256]{1,0:T(8,128)(2,1)S(1)}, bf16[512,256]{1,0:T(8,128)(2,1)S(1)}, u32[]{:S(2)}, u32[]{:S(2)}) collective-permute-start(bf16[512,256]{1,0:T(8,128)(2,1)S(1)} %add_convert_fusion), channel_id=1, source_target_pairs={{0,60},{1,5},{2,62},{3,7},{4,0},{5,9},{6,2},{7,11},{8,4},{9,13},{1... | collective-permute-start | bytes 786440 | tf_op jit(solution)/shard_map/ppermute | solution.py:20

commit v5 on v4

--- a/solution.py
+++ b/solution.py
@@ -6,6 +6,7 @@
 from jax.sharding import Mesh
 from jax.sharding import PartitionSpec as P
 
+
 Z = ("zo", "zi")
 TENSOR = ("zo", "zi", "core")
 F32 = jnp.float32
@@ -34,38 +35,49 @@
 
 
 def vmem_call(kernel, outs, *args, flops, scratch=()):
-    size = sum(a.size * a.dtype.itemsize for a in (*args, *jax.tree.leaves(outs)))
+    vmem = pl.BlockSpec(memory_space=pltpu.VMEM)
+    flat, tree = jax.tree.flatten(args)
+    size = sum(a.size * a.dtype.itemsize for a in (*flat, *jax.tree.leaves(outs)))
+
+    def body(*refs):
+        kernel(*jax.tree.unflatten(tree, refs[: len(flat)]), *refs[len(flat) :])
+
     return pl.pallas_call(
-        kernel,
+        body,
         out_shape=outs,
-        in_specs=[pl.BlockSpec(memory_space=pltpu.VMEM)] * len(args),
-        out_specs=jax.tree.map(lambda _: pl.BlockSpec(memory_space=pltpu.VMEM), outs),
+        in_specs=[vmem] * len(flat),
+        out_specs=jax.tree.map(lambda _: vmem, outs),
         scratch_shapes=scratch,
         compiler_params=pltpu.CompilerParams(vmem_limit_bytes=40 * 2**20),
         cost_estimate=pl.CostEstimate(flops=flops, bytes_accessed=size, transcendentals=0),
-    )(*args)
-
-
-def product(pair_ref, weight_ref, residue):
-    blocks = [jnp.concatenate([pair_ref[k], pair_ref[k + 1]], axis=1) for k in range(0, pair_ref.shape[0], 2)]
-    pair = jnp.concatenate(blocks)
-    width = pair.shape[1]
-    return jnp.dot(pair, weight_ref[whole(residue * width, width), :], preferred_element_type=F32)
-
-
-def near_kernel(own_ref, *refs):
-    side_refs, weight_ref, total_ref = refs[:-2], refs[-2], refs[-1]
-    core = lax.axis_index("core")
-    total_ref[...] = product(own_ref, weight_ref, lax.axis_index("zi"))
-    for step, ref in zip(STEPS, side_refs):
-        total_ref[...] += product(ref, weight_ref, residue_at(step, core))
+    )(*flat)
+
+
+def add_product(total, ref, at, half, weight_ref, residue):
+    blocks = range(at, at + lax.axis_size("dp"), 2)
+    data = jnp.concatenate([jnp.concatenate([ref[k], ref[k + 1]], axis=1) for k in blocks])
+    rows, width = data.shape
+    weight = weight_ref[whole(residue * width, width), :]
+    total[whole(half * rows, rows), :] += jnp.dot(data, weight, preferred_element_type=F32)
+
+
+def near_kernel(own_ref, one_ref, two_refs, three_refs, four_ref, weight_ref, total):
+    core, n = lax.axis_index("core"), lax.axis_size("dp")
+    total[...] = jnp.zeros_like(total)
+    for half in (0, 1):
+        add_product(total, own_ref, half * n, half, weight_ref, lax.axis_index("zi"))
+        add_product(total, one_ref, half * n, half, weight_ref, residue_at(1, core))
+    for step, refs in ((2, two_refs), (3, three_refs), (4, (four_ref,))):
+        for ref, half in zip(refs, (core, 1 - core)):
+            add_product(total, ref, 0, half, weight_ref, residue_at(step, core))
 
 
 def up_kernel(total_in_ref, theirs_ref, weight_ref, out_ref, rest_ref, total):
-    core = lax.axis_index("core")
+    core, n = lax.axis_index("core"), lax.axis_size("dp")
     total[...] = total_in_ref[...]
-    for k, step in enumerate(STEPS):
-        total[...] += product(theirs_ref.at[k], weight_ref, residue_at(step, 1 - core))
+    halves = (1, 0), (1, 1), (2, 1 - core), (2, core), (3, 1 - core), (3, core), (4, 1 - core)
+    for k, (step, half) in enumerate(halves):
+        add_product(total, theirs_ref, k * n, half, weight_ref, residue_at(step, 1 - core))
     columns = total.shape[1]
     row = lax.broadcasted_iota(jnp.int32, (columns, columns), 0)
     col = lax.broadcasted_iota(jnp.int32, (columns, columns), 1)
@@ -127,18 +139,27 @@
     copies = lax.all_to_all(copies, "zo", split_axis=0, concat_axis=0, tiled=True)
     copies = jnp.repeat(copies, 2, axis=0)
     pair = lax.all_to_all(copies, ("dp", "core"), split_axis=0, concat_axis=0, tiled=True)
-    two = shifted(pair, 2)
+    core = lax.axis_index("core")
+    halves = pair.reshape(2, dp, rows, width)
+    first = jnp.where(core == 0, halves[0], halves[1])
+    second = jnp.where(core == 0, halves[1], halves[0])
+    first, second, pair = lax.optimization_barrier((first, second, pair))
+    first = shifted(first, 2)
+    second = shifted(second, 2)
     one = shifted(pair, 1)
-    two, other_weight = lax.optimization_barrier((two, other_weight))
-    four = shifted(two, 2, cores=(1,))
-    three = shifted(two, 1)
-    side = (one, two, three, four)
-    theirs = swapped(jnp.stack(side))
+    first, other_weight = lax.optimization_barrier((first, other_weight))
+    four = shifted(first, 2)
+    two = (first, second)
+    three = (shifted(first, 1), shifted(second, 1))
+    theirs = swapped(jnp.concatenate([one, *two, *three, four]))
     total = vmem_call(
         near_kernel,
         shape((dp * rows, columns), F32),
         pair,
-        *side,
+        one,
+        two,
+        three,
+        four,
         gate_up_weight,
         flops=dp * rows * gate_up_weight.size,
     )

time: 213 us -> 216 us (1.014)
  the two profiles are of different devices: /device:TPU:104 before, /device:TPU:40 now
where the time goes in v5:
time: 216 us
  starting transfers between devices  78.8 us (36%)
  blocking collectives  73 us (34%)
  waiting for transfers between devices  57.3 us (27%)
  Pallas kernels  3 us (1%)
  local copies, waits for them, and re-layouts  2.48 us (1%)
    all_to_all x1, starting transfers between devices, per_device(): lax.all_to_all(copies, 'zo', split_axis=0, concat_axis=0, tiled=True)  43 us
    all_to_all x1, blocking collectives, per_device(): out = lax.all_to_all(out, 'zo', split_axis=0, concat_axis=0, tiled=True)  32.8 us
    all_to_all x1, waiting for transfers between devices, per_device(): lax.all_to_all(copies, 'zo', split_axis=0, concat_axis=0, tiled=True)  27.8 us
    ppermute x10, starting transfers between devices, shifted(): return lax.ppermute(array, TENSOR, pairs)  27.3 us
    ppermute x10, waiting for transfers between devices, shifted(): return lax.ppermute(array, TENSOR, pairs)  20.3 us
    all_to_all x1, blocking collectives, per_device(): parts = lax.all_to_all(parts, 'dp', split_axis=0, concat_axis=0, tiled=True)  12.6 us
    all_to_all x1, blocking collectives, per_device(): lax.all_to_all(hidden, 'dp', split_axis=0, concat_axis=0, tiled=True)  9.1 us
    all_to_all x1, blocking collectives, per_device(): out = lax.all_to_all(out, 'dp', split_axis=0, concat_axis=0, tiled=True)  8.5 us
  transfers between devices with their start and end apart: 14, of which 8 were waited for; matrix products, arithmetic and copies ran while one was open for 0% of the time, Pallas kernels for 0%

profile of v5, /device:TPU:40, one launch (start us, length us, event | category | flops | bytes accessed | tf_op | source)
XLA Modules:
  0.0 215.5 jit_solution(17821705672166566119)
XLA Ops:
  0.0 0.0 copy-start
  0.0 1.6 broadcast_in_dim.6
  1.6 43.0 %all-to-all-start = ((bf16[4,128,128]{2,1,0:T(8,128)(2,1)}), bf16[4,128,128]{2,1,0:T(8,128)(2,1)S(1)}, u32[]{:S(2)}, u32[]{:S(2)}) async-start(bf16[4,128,128]{2,1,0:T(8,128)(2,1)} %broadcast_in_dim.6), calls=%async_computation | async-start | bytes 262144 | tf_op jit(solution)/shard_map/all_to_all | solution.py:139
  44.6 1.9 collective-permute-start.2
  46.5 27.8 %all-to-all-done = bf16[4,128,128]{2,1,0:T(8,128)(2,1)S(1)} async-done(((bf16[4,128,128]{2,1,0:T(8,128)(2,1)}), bf16[4,128,128]{2,1,0:T(8,128)(2,1)S(1)}, u32[]{:S(2)}, u32[]{:S(2)}) %all-to-all-start) | async-done | bytes 131104 | tf_op jit(solution)/shard_map/all_to_all | solution.py:139
  74.4 0.7 broadcast_in_dim.7
  75.1 4.6 %all-to-all-start.1 = ((bf16[8,128,128]{2,1,0:T(8,128)(2,1)}), bf16[8,128,128]{2,1,0:T(8,128)(2,1)S(1)}, u32[]{:S(2)}, u32[]{:S(2)}) async-start(bf16[8,128,128]{2,1,0:T(8,128)(2,1)} %bitcast.9), calls=%async_computation.1 | async-start | bytes 524288 | tf_op jit(solution)/shard_map/all_to_all | solution.py:141
  79.7 7.5 %all-to-all-done.1.refs_0_ = bf16[8,128,128]{2,1,0:T(8,128)(2,1)S(1)} async-done(((bf16[8,128,128]{2,1,0:T(8,128)(2,1)}), bf16[8,128,128]{2,1,0:T(8,128)(2,1)S(1)}, u32[]{:S(2)}, u32[]{:S(2)}) %all-to-all-start.1) | async-done | bytes 262176 | tf_op jit(solution)/shard_map/all_to_all | solution.py:141
  87.2 2.0 collective-permute-start
  89.2 2.0 collective-permute-start.1
  91.1 4.7 %collective-permute-start.3 = (bf16[4,128,128]{2,1,0:T(8,128)(2,1)S(1)}, bf16[4,128,128]{2,1,0:T(8,128)(2,1)S(1)}, u32[]{:S(2)}, u32[]{:S(2)}) collective-permute-start(bf16[4,128,128]{2,1,0:T(8,128)(2,1)S(1)} %get-tuple-element.20), channel_id=1, source_target_pairs={{0,4},{1,61},{2,6},{3,63},{4,8},{5,1},{6,10},{7,3},{8,12},{9,5},{1... | collective-permute-start | bytes 393224 | tf_op jit(solution)/shard_map/ppermute | solution.py:21
  95.9 0.0 collective-permute-done.2.refs_2_
  95.9 6.8 %collective-permute-done.1.refs_2_ = bf16[4,128,128]{2,1,0:T(8,128)(2,1)S(1)} collective-permute-done((bf16[4,128,128]{2,1,0:T(8,128)(2,1)S(1)}, bf16[4,128,128]{2,1,0:T(8,128)(2,1)S(1)}, u32[]{:S(2)}, u32[]{:S(2)}) %collective-permute-start.1) | collective-permute-done | bytes 131104 | tf_op jit(solution)/shard_map/ppermute | solution.py:21
  102.7 1.9 collective-permute-start.6
  104.6 2.0 collective-permute-start.4
  106.6 0.0 collective-permute-done.3.refs_3_
  106.6 2.0 collective-permute-start.5
  108.6 0.0 collective-permute-done.refs_1_
  108.7 4.4 %collective-permute-done.4.refs_4_ = bf16[4,128,128]{2,1,0:T(8,128)(2,1)S(1)} collective-permute-done((bf16[4,128,128]{2,1,0:T(8,128)(2,1)S(1)}, bf16[4,128,128]{2,1,0:T(8,128)(2,1)S(1)}, u32[]{:S(2)}, u32[]{:S(2)}) %collective-permute-start.4) | collective-permute-done | bytes 131104 | tf_op jit(solution)/shard_map/ppermute | solution.py:21
  113.1 1.6 collective-permute-done.5.refs_5_
  114.7 0.0 collective-permute-done.6.refs_6_
  114.8 2.0 collective-permute-start.7
  116.7 0.0 copy-done
  116.7 0.8 shard_map.37.refs_0_
  117.5 1.6 collective-permute-done.7.refs_1_
  119.2 1.1 shard_map.38
  120.3 0.0 copy-start.1
  120.3 12.6 %all_to_all.30.refs_0_ = bf16[4,128,512]{2,1,0:T(8,128)(2,1)S(1)} all-to-all(bf16[4,128,512]{2,1,0:T(8,128)(2,1)S(1)} %bitcast.6), channel_id=1, replica_groups=mesh['groups'=2,'dp'=4,'zo'=4,'zi'=8,'core'=2] {'dp'}, dimensions={0} | all-to-all | bytes 1048576 | tf_op jit(solution)/shard_map/all_to_all | solution.py:176
  133.0 0.1 shard_map.39
  133.1 9.1 %all_to_all.31 = bf16[4,128,256]{2,1,0:T(8,128)(2,1)S(1)} all-to-all(bf16[4,128,256]{2,1,0:T(8,128)(2,1)S(1)} %broadcast_in_dim.8), channel_id=1, replica_groups=mesh['groups'=2,'dp'=4,'zo'=4,'zi'=8,'core'=2] {'dp'}, dimensions={0} | all-to-all | bytes 524288 | tf_op jit(solution)/shard_map/all_to_all | solution.py:181
  142.2 2.2 %all_gather.9.refs_0_ = bf16[2,512,256]{2,1,0:T(8,128)(2,1)S(1)} all-gather(bf16[1,512,256]{2,1,0:T(8,128)(2,1)S(1)} %bitcast.8), channel_id=1, replica_groups=mesh['groups'=2,'dp'=4,'zo'=4,'zi'=8,'core'=2] {'core'}, dimensions={0}, use_global_device_ids=true | all-gather | bytes 786432 | tf_op jit(solution)/shard_map/all_gather | solution.py:182
  144.4 0.0 copy-done.1
  144.4 0.9 shard_map.40
  145.3 4.0 %collective-permute-start.9 = (bf16[512,256]{1,0:T(8,128)(2,1)S(1)}, bf16[512,256]{1,0:T(8,128)(2,1)S(1)}, u32[]{:S(2)}, u32[]{:S(2)}) collective-permute-start(bf16[512,256]{1,0:T(8,128)(2,1)S(1)} %get-tuple-element.27), channel_id=1, source_target_pairs={{0,62},{1,3},{2,0},{3,5},{4,2},{5,7},{6,4},{7,9},{8,6},{9,11},{10,... | collective-permute-start | bytes 786440 | tf_op jit(solution)/shard_map/ppermute | solution.py:21
  149.2 0.7 collective-permute-start.10
  149.9 3.4 %collective-permute-start.8 = (bf16[512,256]{1,0:T(8,128)(2,1)S(1)}, bf16[512,256]{1,0:T(8,128)(2,1)S(1)}, u32[]{:S(2)}, u32[]{:S(2)}) collective-permute-start(bf16[512,256]{1,0:T(8,128)(2,1)S(1)} %get-tuple-element.25), channel_id=1, source_target_pairs={{0,62},{1,3},{2,0},{3,5},{4,2},{5,7},{6,4},{7,9},{8,6},{9,11},{10,... | collective-permute-start | bytes 786440 | tf_op jit(solution)/shard_map/ppermute | solution.py:21
  153.3 0.2 collective-permute-done.9
  153.6 0.0 collective-permute-done.10
  153.6 0.1 add_convert_fusion
  153.7 4.8 %collective-permute-start.11 = (bf16[512,256]{1,0:T(8,128)(2,1)S(1)}, bf16[512,256]{1,0:T(8,128)(2,1)S(1)}, u32[]{:S(2)}, u32[]{:S(2)}) collective-permute-start(bf16[512,256]{1,0:T(8,128)(2,1)S(1)} %add_convert_fusion), channel_id=1, source_target_pairs={{0,60},{1,5},{2,62},{3,7},{4,0},{5,9},{6,2},{7,11},{8,4},{9,13},{1... | collective-permute-start | bytes 786440 | tf_op jit(solution)/shard_map/ppermute | solution.py:21
  158.5 0.0 collective-permute-done.8.refs_0_.refs_1_
  158.5 7.2 %collective-permute-done.11.refs_1_.refs_2_ = bf16[512,256]{1,0:T(8,128)(2,1)S(1)} collective-permute-done((bf16[512,256]{1,0:T(8,128)(2,1)S(1)}, bf16[512,256]{1,0:T(8,128)(2,1)S(1)}, u32[]{:S(2)}, u32[]{:S(2)}) %collective-permute-start.11) | collective-permute-done | bytes 262176 | tf_op jit(solution)/shard_map/ppermute | solution.py:21
  165.7 7.8 %all-gather = f32[1024,128]{1,0:T(8,128)S(1)} all-gather(f32[512,128]{1,0:T(8,128)S(1)} %shard_map.41), channel_id=2, replica_groups=mesh['groups'=2,'dp'=4,'zo'=4,'zi'=8,'core'=2] {'core'}, dimensions={0}, use_global_device_ids=true | all-gather | bytes 786432 | tf_op jit(solution)/shard_map/all_gather | solution.py:198
  173.6 0.1 shard_map.42
  173.6 8.5 %all_to_all.32 = bf16[4,128,128]{2,1,0:T(8,128)(2,1)S(1)} all-to-all(bf16[4,128,128]{2,1,0:T(8,128)(2,1)S(1)} %bitcast.7), channel_id=1, replica_groups=mesh['groups'=2,'dp'=4,'zo'=4,'zi'=8,'core'=2] {'dp'}, dimensions={0} | all-to-all | bytes 262144 | tf_op jit(solution)/shard_map/all_to_all | solution.py:201
  182.1 32.8 %all_to_all.33 = bf16[4,128,128]{2,1,0:T(8,128)(2,1)S(1)} all-to-all(bf16[4,128,128]{2,1,0:T(8,128)(2,1)S(1)} %all_to_all.32), channel_id=1, replica_groups=mesh['groups'=2,'dp'=4,'zo'=4,'zi'=8,'core'=2] {'zo'}, dimensions={0} | all-to-all | bytes 262144 | tf_op jit(solution)/shard_map/all_to_all | solution.py:202
  214.9 0.6 reduce_sum.12
  (9 shorter events, 0.2 us)
Async XLA Ops:
  0.0 116.7 %copy-start = (bf16[2048,512]{1,0:T(8,128)(2,1)S(1)}, bf16[2048,512]{1,0:T(8,128)(2,1)}, u32[]{:S(2)}) copy-start(bf16[2048,512]{1,0:T(8,128)(2,1)} %refs_2_.1) | copy-start | bytes 6291460
  1.6 72.8 %all-to-all-start = ((bf16[4,128,128]{2,1,0:T(8,128)(2,1)}), bf16[4,128,128]{2,1,0:T(8,128)(2,1)S(1)}, u32[]{:S(2)}, u32[]{:S(2)}) async-start(bf16[4,128,128]{2,1,0:T(8,128)(2,1)} %broadcast_in_dim.6), calls=%async_computation | async-start | bytes 262144 | tf_op jit(solution)/shard_map/all_to_all | solution.py:139
  44.6 51.3 %collective-permute-start.2 = (bf16[256,2048]{1,0:T(8,128)(2,1)}, bf16[256,2048]{1,0:T(8,128)(2,1)S(1)}, u32[]{:S(2)}, u32[]{:S(2)}) collective-permute-start(bf16[256,2048]{1,0:T(8,128)(2,1)} %refs_1_.1), channel_id=1, source_target_pairs={{0,1},{1,0},{2,3},{3,2},{4,5},{5,4},{6,7},{7,6},{8,9},{9,8},{10,11... | collective-permute-start | bytes 3145736 | tf_op jit(solution)/shard_map/ppermute | solution.py:34
  75.1 12.1 %all-to-all-start.1 = ((bf16[8,128,128]{2,1,0:T(8,128)(2,1)}), bf16[8,128,128]{2,1,0:T(8,128)(2,1)S(1)}, u32[]{:S(2)}, u32[]{:S(2)}) async-start(bf16[8,128,128]{2,1,0:T(8,128)(2,1)} %bitcast.9), calls=%async_computation.1 | async-start | bytes 524288 | tf_op jit(solution)/shard_map/all_to_all | solution.py:141
  87.2 21.4 %collective-permute-start = (bf16[8,128,128]{2,1,0:T(8,128)(2,1)S(1)}, bf16[8,128,128]{2,1,0:T(8,128)(2,1)S(1)}, u32[]{:S(2)}, u32[]{:S(2)}) collective-permute-start(bf16[8,128,128]{2,1,0:T(8,128)(2,1)S(1)} %all-to-all-done.1.refs_0_), channel_id=1, source_target_pairs={{0,2},{1,63},{2,4},{3,1},{4,6},{5,3},{6,8},{7,5},{8,10},{9,7},{10,... | collective-permute-start | bytes 786440 | tf_op jit(solution)/shard_map/ppermute | solution.py:21
  89.2 13.5 %collective-permute-start.1 = (bf16[4,128,128]{2,1,0:T(8,128)(2,1)S(1)}, bf16[4,128,128]{2,1,0:T(8,128)(2,1)S(1)}, u32[]{:S(2)}, u32[]{:S(2)}) collective-permute-start(bf16[4,128,128]{2,1,0:T(8,128)(2,1)S(1)} %get-tuple-element.18), channel_id=1, source_target_pairs={{0,4},{1,61},{2,6},{3,63},{4,8},{5,1},{6,10},{7,3},{8,12},{9,5},{1... | collective-permute-start | bytes 393224 | tf_op jit(solution)/shard_map/ppermute | solution.py:21
  91.1 15.5 %collective-permute-start.3 = (bf16[4,128,128]{2,1,0:T(8,128)(2,1)S(1)}, bf16[4,128,128]{2,1,0:T(8,128)(2,1)S(1)}, u32[]{:S(2)}, u32[]{:S(2)}) collective-permute-start(bf16[4,128,128]{2,1,0:T(8,128)(2,1)S(1)} %get-tuple-element.20), channel_id=1, source_target_pairs={{0,4},{1,61},{2,6},{3,63},{4,8},{5,1},{6,10},{7,3},{8,12},{9,5},{1... | collective-permute-start | bytes 393224 | tf_op jit(solution)/shard_map/ppermute | solution.py:21
  102.7 12.0 %collective-permute-start.6 = (bf16[4,128,128]{2,1,0:T(8,128)(2,1)S(1)}, bf16[4,128,128]{2,1,0:T(8,128)(2,1)S(1)}, u32[]{:S(2)}, u32[]{:S(2)}) collective-permute-start(bf16[4,128,128]{2,1,0:T(8,128)(2,1)S(1)} %collective-permute-done.1.refs_2_), channel_id=1, source_target_pairs={{0,4},{1,61},{2,6},{3,63},{4,8},{5,1},{6,10},{7,3},{8,12},{9,5},{1... | collective-permute-start | bytes 393224 | tf_op jit(solution)/shard_map/ppermute | solution.py:21
  104.6 8.4 %collective-permute-start.4 = (bf16[4,128,128]{2,1,0:T(8,128)(2,1)S(1)}, bf16[4,128,128]{2,1,0:T(8,128)(2,1)S(1)}, u32[]{:S(2)}, u32[]{:S(2)}) collective-permute-start(bf16[4,128,128]{2,1,0:T(8,128)(2,1)S(1)} %collective-permute-done.1.refs_2_), channel_id=1, source_target_pairs={{0,2},{1,63},{2,4},{3,1},{4,6},{5,3},{6,8},{7,5},{8,10},{9,7},{10,... | collective-permute-start | bytes 393224 | tf_op jit(solution)/shard_map/ppermute | solution.py:21
  106.6 8.1 %collective-permute-start.5 = (bf16[4,128,128]{2,1,0:T(8,128)(2,1)S(1)}, bf16[4,128,128]{2,1,0:T(8,128)(2,1)S(1)}, u32[]{:S(2)}, u32[]{:S(2)}) collective-permute-start(bf16[4,128,128]{2,1,0:T(8,128)(2,1)S(1)} %collective-permute-done.3.refs_3_), channel_id=1, source_target_pairs={{0,2},{1,63},{2,4},{3,1},{4,6},{5,3},{6,8},{7,5},{8,10},{9,7},{10,... | collective-permute-start | bytes 393224 | tf_op jit(solution)/shard_map/ppermute | solution.py:21
  114.8 4.4 %collective-permute-start.7 = (bf16[28,128,128]{2,1,0:T(8,128)(2,1)S(1)}, bf16[28,128,128]{2,1,0:T(8,128)(2,1)S(1)}, u32[]{:S(2)}, u32[]{:S(2)}) collective-permute-start(bf16[28,128,128]{2,1,0:T(8,128)(2,1)S(1)} %constant_dynamic-update-slice_fusion), channel_id=1, source_target_pairs={{0,1},{1,0},{2,3},{3,2},{4,5},{5,4},{6,7},{7,6},{8,9},{9,8},{10,11... | collective-permute-start | bytes 2752520 | tf_op jit(solution)/shard_map/ppermute | solution.py:34
  120.3 24.1 %copy-start.1 = (bf16[256,2048]{1,0:T(8,128)(2,1)S(1)}, bf16[256,2048]{1,0:T(8,128)(2,1)}, u32[]{:S(2)}) copy-start(bf16[256,2048]{1,0:T(8,128)(2,1)} %refs_1_.1) | copy-start | bytes 3145732
  145.3 8.3 %collective-permute-start.9 = (bf16[512,256]{1,0:T(8,128)(2,1)S(1)}, bf16[512,256]{1,0:T(8,128)(2,1)S(1)}, u32[]{:S(2)}, u32[]{:S(2)}) collective-permute-start(bf16[512,256]{1,0:T(8,128)(2,1)S(1)} %get-tuple-element.27), channel_id=1, source_target_pairs={{0,62},{1,3},{2,0},{3,5},{4,2},{5,7},{6,4},{7,9},{8,6},{9,11},{10,... | collective-permute-start | bytes 786440 | tf_op jit(solution)/shard_map/ppermute | solution.py:21
  149.2 4.3 %collective-permute-start.10 = (bf16[512,256]{1,0:T(8,128)(2,1)S(1)}, bf16[512,256]{1,0:T(8,128)(2,1)S(1)}, u32[]{:S(2)}, u32[]{:S(2)}) collective-permute-start(bf16[512,256]{1,0:T(8,128)(2,1)S(1)} %get-tuple-element.28), channel_id=1, source_target_pairs={{1,5},{3,7},{5,9},{7,11},{9,13},{11,15},{13,17},{15,19},{17,21},{1... | collective-permute-start | bytes 786440 | tf_op jit(solution)/shard_map/ppermute | solution.py:21
  149.9 8.6 %collective-permute-start.8 = (bf16[512,256]{1,0:T(8,128)(2,1)S(1)}, bf16[512,256]{1,0:T(8,128)(2,1)S(1)}, u32[]{:S(2)}, u32[]{:S(2)}) collective-permute-start(bf16[512,256]{1,0:T(8,128)(2,1)S(1)} %get-tuple-element.25), channel_id=1, source_target_pairs={{0,62},{1,3},{2,0},{3,5},{4,2},{5,7},{6,4},{7,9},{8,6},{9,11},{10,... | collective-permute-start | bytes 786440 | tf_op jit(solution)/shard_map/ppermute | solution.py:21
  153.7 12.0 %collective-permute-start.11 = (bf16[512,256]{1,0:T(8,128)(2,1)S(1)}, bf16[512,256]{1,0:T(8,128)(2,1)S(1)}, u32[]{:S(2)}, u32[]{:S(2)}) collective-permute-start(bf16[512,256]{1,0:T(8,128)(2,1)S(1)} %add_convert_fusion), channel_id=1, source_target_pairs={{0,60},{1,5},{2,62},{3,7},{4,0},{5,9},{6,2},{7,11},{8,4},{9,13},{1... | collective-permute-start | bytes 786440 | tf_op jit(solution)/shard_map/ppermute | solution.py:21
